TPU v7x, 8 devices: a whole 2x2x1 slice. The times are simulated.
8 devices in a mesh: replica: 1 (over z), model: 8 (over y, x, core).
Axes of the slice: x: 2, y: 2, z: 1, core: 2. Of those that a mesh axis runs over, the one named last changes fastest.
Arguments:
- x: bfloat16 [6, 7168], P('replica')
- w_q: bfloat16 [7168, 16384], P(None, 'model')
- w_k: bfloat16 [7168, 256], replicated
- w_v: bfloat16 [7168, 256], replicated
- w_o: bfloat16 [16384, 7168], P('model')
- k_cache: bfloat16 [6, 1, 16384, 256], P('replica', None, 'model')
- v_cache: bfloat16 [6, 1, 16384, 256], P('replica', None, 'model')
- lengths: int32 [6], P('replica')
Outputs:
- output 1: bfloat16 [6, 7168], P('replica')
- output 2: bfloat16 [6, 256], P('replica')
- output 3: bfloat16 [6, 256], P('replica')
All inputs are finite; a program needn't handle non-finite values.
Results may differ from a plain program's by a relative error of at most 0.00765567.
Values are sent between devices in bfloat16 or wider.
A program may use at most 1 GiB of HBM per device.

v0:
```python
import jax
import jax.numpy as jnp
from jax import lax
from jax.sharding import PartitionSpec as P, NamedSharding


def solution(mesh):
    n_dev = mesh.shape['model']

    def local_step(x, w_q, w_k, w_v, w_o, k_cache, v_cache, lengths):
        rows, kv_heads, t_local, head_dim = k_cache.shape
        col_local = w_q.shape[1]
        heads = col_local * n_dev // head_dim
        group = heads // kv_heads
        scale = head_dim ** -0.5
        shard = lax.axis_index('model')
        q_local = jnp.dot(x, w_q, preferred_element_type=jnp.float32).astype(jnp.bfloat16)
        q_all = lax.all_gather(q_local, 'model', axis=1, tiled=True)
        k_new = jnp.dot(x, w_k, preferred_element_type=jnp.float32).astype(jnp.bfloat16)
        v_new = jnp.dot(x, w_v, preferred_element_type=jnp.float32).astype(jnp.bfloat16)
        q_heads = q_all.reshape(rows, kv_heads, group, head_dim)
        scores = jnp.einsum('bkgd,bktd->bkgt', q_heads, k_cache, preferred_element_type=jnp.float32) * scale
        positions = shard * t_local + jnp.arange(t_local)
        valid = positions[None, :] < lengths[:, None]
        scores = jnp.where(valid[:, None, None, :], scores, -jnp.inf)
        score_new = jnp.einsum('clhe,cle->clh', q_heads, k_new.reshape(rows, kv_heads, head_dim), preferred_element_type=jnp.float32) * scale
        top = jnp.maximum(lax.pmax(jnp.max(scores, axis=-1), 'model'), score_new)
        weights = jnp.exp(scores - top[..., None])
        weight_new = jnp.exp(score_new - top)
        total = lax.psum(jnp.sum(weights, axis=-1), 'model') + weight_new
        part_out = jnp.einsum('bkgt,bktd->bkgd', weights, v_cache, preferred_element_type=jnp.float32)
        part_out = (part_out / total[..., None]).reshape(rows, heads * head_dim)
        own_out = lax.psum_scatter(part_out, 'model', scatter_dimension=1, tiled=True)
        new_term = (weight_new / total)[..., None] * v_new.reshape(rows, kv_heads, 1, head_dim).astype(jnp.float32)
        new_term = lax.dynamic_slice_in_dim(new_term.reshape(rows, heads * head_dim), shard * col_local, col_local, axis=1)
        attn_local = (own_out + new_term).astype(jnp.bfloat16)
        y_part = jnp.dot(attn_local, w_o, preferred_element_type=jnp.float32)
        y_out = (x.astype(jnp.float32) + lax.psum(y_part, 'model')).astype(jnp.bfloat16)
        return y_out, k_new, v_new

    row_spec = P('replica', None)
    cache_spec = P('replica', None, 'model', None)
    return jax.shard_map(local_step, mesh=mesh, in_specs=(row_spec, P(None, 'model'), P(), P(), P('model', None), cache_spec, cache_spec, P('replica')), out_specs=(row_spec, row_spec, row_spec), check_vma=False)
```

profile of v0, /device:TPU:0, one launch (start us, length us, event | category | flops | bytes accessed | tf_op | source)
XLA Modules:
  0.0 183.9 jit_solution(17479320261826795426)
XLA Ops:
  7.2 0.0 reduce-scatter.2.cloned.1.call-start
  7.2 0.0 copy-start.3
  7.2 0.0 copy-start
  7.2 13.4 %convolution_convert_fusion = bf16[6,2048]{1,0:T(8,128)(2,1)S(1)} fusion(bf16[6,7168]{1,0:T(8,128)(2,1)} %param.8, bf16[7168,2048]{1,0:T(8,128)(2,1)} %param.9), kind=kOutput, calls=%fused_computation.7 | convolution fusion | flops 176173056 | bytes 29470720 | tf_op jit(solution)/shard_map/dot_general | solution.py:17
  20.7 14.4 %all_gather.3 = bf16[6,16384]{1,0:T(8,128)(2,1)S(1)} all-gather(bf16[6,2048]{1,0:T(8,128)(2,1)S(1)} %convolution_convert_fusion), channel_id=1, replica_groups=mesh['replica'=1,'model'=8] {'model'}, dimensions={1}, use_global_device_ids=true | all-gather | bytes 221184 | tf_op jit(solution)/shard_map/all_gather | solution.py:18
  35.1 0.0 copy-done.3
  35.1 0.1 broadcast_compare_fusion
  35.2 0.0 copy-done
  35.2 0.0 copy-start.1
  35.2 2.1 %fusion.24 = (f32[6,64]{1,0:T(8,128)S(1)}, f32[6,64,2048]{2,1,0:T(8,128)S(1)}) fusion(bf16[6,1,2048,256]{3,2,1,0:T(8,128)(2,1)S(1)} %copy-done, bf16[1,6,64,256]{3,1,2,0:T(8,128)(2,1)S(1)} %bitcast.72, pred[6,2048]{1,0:T(8,128)(4,1)S(1)} %broadcast_compare_fusion), kind=kOutput, calls=%fused_computation.33 | convolution fusion | flops 405012096 | bytes 9647616 | tf_op jit(solution)/shard_map/bkgd,bktd->bkgt/dot_general | solution.py:22
  37.3 22.3 %pmax.7 = f32[6,1,64]{2,0,1:T(8,128)S(1)} all-reduce(f32[6,1,64]{2,0,1:T(8,128)S(1)} %bitcast.75), channel_id=1, replica_groups=mesh['replica'=1,'model'=8] {'model'}, use_global_device_ids=true, to_apply=%region_1.2 | all-reduce | flops 384 | bytes 3072 | tf_op jit(solution)/shard_map/pmax | solution.py:27
  59.6 0.0 copy-done.1
  59.6 2.6 %convolution_convert_fusion.2 = bf16[6,256]{1,0:T(8,128)(2,1)S(1)} fusion(bf16[6,7168]{1,0:T(8,128)(2,1)S(1)} %copy-done.1, bf16[7168,256]{1,0:T(8,128)(2,1)} %param.10), kind=kOutput, calls=%fused_computation.12 | convolution fusion | flops 22021632 | bytes 3759104 | tf_op jit(solution)/shard_map/dot_general | solution.py:19
  62.2 0.0 copy-start.2
  62.2 0.2 fusion.14
  62.4 0.6 fusion.6
  62.9 23.1 %psum.14 = f32[6,1,64]{2,0,1:T(8,128)S(1)} all-reduce(f32[6,1,64]{2,0,1:T(8,128)S(1)} %bitcast.76), channel_id=1, replica_groups=mesh['replica'=1,'model'=8] {'model'}, use_global_device_ids=true, to_apply=%region_3.4 | all-reduce | flops 384 | bytes 3072 | tf_op jit(solution)/shard_map/psum | solution.py:30
  86.0 4.0 %fusion.11 = f32[1,6,64,256]{3,2,1,0:T(8,128)S(1)} fusion(bf16[6,1,2048,256]{3,2,1,0:T(8,128)(2,1)} %param.14, f32[6,64,2048]{2,1,0:T(8,128)S(1)} %get-tuple-element.6, f32[6,64]{1,0:T(8,128)S(1)} %fusion.22, f32[6,64]{1,0:T(8,128)S(1)} %get-tuple-element.4), kind=kOutput, calls=%fused_computation.10 | convolution fusion | flops 403537920 | bytes 9833472 | tf_op jit(solution)/shard_map/bkgt,bktd->bkgd/dot_general | solution.py:31
  90.0 0.0 copy-done.2
  90.0 1.0 copy.14
  91.1 0.0 reduce-scatter.2.cloned.1.call-update
  91.1 0.2 all-reduce.2.cloned.1.call-start
  91.3 3.2 %fusion.25 = (f32[6,256]{1,0:T(8,128)S(1)}, bf16[6,256]{1,0:T(8,128)(2,1)}) fusion(bf16[6,7168]{1,0:T(8,128)(2,1)S(1)} %copy-done.1, bf16[7168,256]{1,0:T(8,128)(2,1)} %param.11), kind=kOutput, calls=%fused_computation.34 | convolution fusion | flops 22023168 | bytes 3765248 | tf_op jit(solution)/shard_map/dot_general | solution.py:20
  94.5 0.1 multiply_bitcast_fusion
  94.7 0.2 copy.15
  94.9 23.9 %reduce-scatter.2.cloned.1.call-done = f32[6,2048]{1,0:T(8,128)} async-done(((f32[6,16384]{1,0:T(8,128)}), f32[6,2048]{1,0:T(8,128)}) %reduce-scatter.2.cloned.1.call-update) | async-done | bytes 49168 | tf_op jit(solution)/shard_map/reduce_scatter | solution.py:33
  118.8 14.0 %fusion.19 = f32[6,7168]{1,0:T(8,128)} fusion(bf16[2048,7168]{1,0:T(8,128)(2,1)} %param.12, f32[6,2048]{1,0:T(8,128)} %reduce-scatter.2.cloned.1.call-done, f32[6,16384]{1,0:T(8,128)S(1)} %bitcast.74, s32[]{:T(128)S(6)} %select_n.9), kind=kOutput, calls=%fused_computation.21 | convolution fusion | flops 176185344 | bytes 29646852 | tf_op jit(solution)/shard_map/dot_general | solution.py:37
  132.8 0.0 all-reduce.2.cloned.1.call-update
  132.8 42.7 %all-reduce.2.cloned.1.call-done = f32[6,7168]{1,0:T(8,128)} async-done(((f32[6,7168]{1,0:T(8,128)}), f32[6,7168]{1,0:T(8,128)}) %all-reduce.2.cloned.1.call-update) | async-done | bytes 172048 | tf_op jit(solution)/shard_map/psum | solution.py:38
  175.5 1.6 add_convert_fusion
  (3 shorter events, 0.0 us)
Async XLA Ops:
  7.2 111.6 %reduce-scatter.2.cloned.1.call-start = ((), (), s32[]{:S(2)}) async-start(), calls=%async_computation.1 | async-start | bytes 589824 | tf_op jit(solution)/shard_map/reduce_scatter | solution.py:33
  7.2 27.9 %copy-start.3 = (s32[6]{0:T(128)S(1)}, s32[6]{0:T(128)}, u32[]{:S(2)}) copy-start(s32[6]{0:T(128)} %param.15) | copy-start | bytes 76
  7.2 27.9 %copy-start = (bf16[6,1,2048,256]{3,2,1,0:T(8,128)(2,1)S(1)}, bf16[6,1,2048,256]{3,2,1,0:T(8,128)(2,1)}, u32[]{:S(2)}) copy-start(bf16[6,1,2048,256]{3,2,1,0:T(8,128)(2,1)} %param.13) | copy-start | bytes 18874372
  35.2 24.4 %copy-start.1 = (bf16[6,7168]{1,0:T(8,128)(2,1)S(1)}, bf16[6,7168]{1,0:T(8,128)(2,1)}, u32[]{:S(2)}) copy-start(bf16[6,7168]{1,0:T(8,128)(2,1)} %param.8) | copy-start | bytes 258052
  62.2 27.8 %copy-start.2 = (bf16[6,256]{1,0:T(8,128)(2,1)}, bf16[6,256]{1,0:T(8,128)(2,1)S(1)}, u32[]{:S(2)}) copy-start(bf16[6,256]{1,0:T(8,128)(2,1)S(1)} %convolution_convert_fusion.2) | copy-start | bytes 9220
  91.1 84.4 %all-reduce.2.cloned.1.call-start = ((), (), s32[]{:S(2)}) async-start(), calls=%async_computation.2 | async-start | bytes 458752 | tf_op jit(solution)/shard_map/psum | solution.py:38
Sparse Core Ops, SparseCore 0:
  91.2 27.5 reduce-scatter.1
  132.9 42.5 all-reduce.1
where the time goes:
time: 184 us
  waiting for transfers between devices  66.6 us (36%)
  blocking collectives  59.7 us (32%)
  matrix products  39.5 us (21%)
  between operations  14.1 us (8%)
  other arithmetic  2.39 us (1%)
    psum x1, waiting for transfers between devices, local_step(): lax.psum(y_part, 'model')  42.7 us
    reduce_scatter x1, waiting for transfers between devices, local_step(): lax.psum_scatter(part_out, 'model', scatter_dimension=1, tiled=True)  23.9 us
    psum x1, blocking collectives, local_step(): total = lax.psum(jnp.sum(weights, axis=-1), 'model') + weight_new  23.1 us
    pmax x1, blocking collectives, local_step(): top = jnp.maximum(lax.pmax(jnp.max(scores, axis=-1), 'model'), score_new)  22.3 us
    all_gather x1, blocking collectives, local_step(): q_all = lax.all_gather(q_local, 'model', axis=1, tiled=True)  14.4 us
    dot_general x1, matrix products, local_step(): y_part = jnp.dot(attn_local, w_o, preferred_element_type=jnp.float32)  14 us
    dot_general x1, matrix products, local_step(): jnp.dot(x, w_q, preferred_element_type=jnp.float32).astype(jnp.bfloat16)  13.4 us
    dot_general x1, matrix products, local_step(): jnp.einsum('bkgt,bktd->bkgd', weights, v_cache, preferred_element_type=jn...  4.02 us
  transfers between devices with their start and end apart: 2, of which 2 were waited for; matrix products, arithmetic and copies ran while one was open for 2% of the time, Pallas kernels for 0%

commit v1 on v0

v1 whole, which is shorter than its diff:
```python
import functools
import math

import jax
import jax.numpy as jnp
from jax import lax
from jax.experimental import pallas as pl
from jax.experimental.pallas import tpu as pltpu
from jax.sharding import PartitionSpec as P

RING = 4
LANES = 128


def peer_of(me, k, n_dev):
    return lax.rem(me + k, n_dev)


def kernel(n_dev, x_hbm, wq_hbm, wk_hbm, wv_hbm, wo_hbm, kc_hbm, vc_hbm, len_ref,
           y_out, k_out, v_out,
           x_v, wq_v, wkv_v, k_v, v_v, wo_v,
           qbuf, kvbuf, osend, obuf, mlsend, mlbuf, astage, a_v, ysend, ybuf, y_v, kvout_v,
           x_sem, wq_sem, wkv_sem, k_sem, v_sem, wo_sem, out_sem,
           q_ssem, q_rsem, kv_ssem, kv_rsem, o_ssem, o_rsem, ml_ssem, ml_rsem,
           y_ssem, y_rsem, g_ssem, g_rsem):
    rows, depth = x_hbm.shape
    head_dim = wk_hbm.shape[1]
    own_heads = wq_hbm.shape[1] // head_dim
    t_local = kc_hbm.shape[2]
    heads = own_heads * n_dev
    kv_rows = depth // n_dev
    y_cols = wo_hbm.shape[1] // n_dev
    me = lax.axis_index("model")
    factor = head_dim ** -0.5 * math.log2(math.e)
    f32, bf16 = jnp.float32, jnp.bfloat16

    def head_cols(h):
        return pl.ds(pl.multiple_of(h * head_dim, head_dim), head_dim)

    def own_cols(p):
        return pl.ds(pl.multiple_of(p * y_cols, LANES), y_cols)

    def wq_copy(h):
        slot = lax.rem(h, RING)
        return pltpu.make_async_copy(wq_hbm.at[:, head_cols(h)], wq_v.at[slot], wq_sem.at[slot])

    def wo_copy(j):
        p = lax.rem(me + 1 + j, n_dev)
        return pltpu.make_async_copy(wo_hbm.at[:, own_cols(p)], wo_v.at[j], wo_sem.at[j])

    kv_slice = pl.ds(pl.multiple_of(me * kv_rows, LANES), kv_rows)
    x_copy = pltpu.make_async_copy(x_hbm, x_v, x_sem)
    wk_copy = pltpu.make_async_copy(wk_hbm.at[kv_slice, :], wkv_v.at[0], wkv_sem.at[0])
    wv_copy = pltpu.make_async_copy(wv_hbm.at[kv_slice, :], wkv_v.at[1], wkv_sem.at[1])

    def k_copy(b):
        return pltpu.make_async_copy(kc_hbm.at[b, 0], k_v.at[b], k_sem.at[b])

    def v_copy(b):
        return pltpu.make_async_copy(vc_hbm.at[b, 0], v_v.at[b], v_sem.at[b])

    x_copy.start()
    for h in range(RING):
        wq_copy(h).start()

    barrier = pltpu.get_barrier_semaphore()
    for k in range(1, n_dev):
        pl.semaphore_signal(barrier, inc=1, device_id={"model": peer_of(me, k, n_dev)},
                            device_id_type=pl.DeviceIdType.MESH)
    pl.semaphore_wait(barrier, n_dev - 1)
    x_copy.wait()

    def send_all(src, dst, ssem, rsem):
        def body(k, c):
            pltpu.make_async_remote_copy(
                src_ref=src, dst_ref=dst, send_sem=ssem, recv_sem=rsem,
                device_id={"model": peer_of(me, k, n_dev)},
                device_id_type=pl.DeviceIdType.MESH).start()
            return c
        lax.fori_loop(1, n_dev, body, 0, unroll=True)

    def wait_bytes(ref, sem):
        pltpu.make_async_copy(ref, ref, sem).wait()

    def q_step(h, c):
        wq_copy(h).wait()
        q = jnp.dot(x_v[...], wq_v[lax.rem(h, RING)], preferred_element_type=f32)
        block = me * own_heads + h
        qbuf[block] = q.astype(bf16).astype(f32)
        send_all(qbuf.at[block], qbuf.at[block], q_ssem, q_rsem)

        @pl.when(h < own_heads - RING)
        def _():
            wq_copy(h + RING).start()

        @pl.when(h == own_heads - RING - 1)
        def _():
            wk_copy.start()
            wv_copy.start()
            for b in range(rows):
                k_copy(b).start()
                v_copy(b).start()
            for j in range(n_dev):
                wo_copy(j).start()
        return c

    lax.fori_loop(0, own_heads, q_step, 0)

    wk_copy.wait()
    wv_copy.wait()
    x_part = x_v[:, kv_slice]
    for i in range(2):
        kvbuf[me, i] = jnp.dot(x_part, wkv_v[i], preferred_element_type=f32)
    send_all(kvbuf.at[me], kvbuf.at[me], kv_ssem, kv_rsem)

    wait_bytes(qbuf.at[pl.ds(0, heads - own_heads)], q_rsem)

    positions = me * t_local + lax.broadcasted_iota(jnp.int32, (1, t_local), 1)
    lane = lax.broadcasted_iota(jnp.int32, (heads, LANES), 1)

    def attend(b, ml):
        k_copy(b).wait()
        q_b = qbuf[:, b, :].astype(bf16)
        s = lax.dot_general(q_b, k_v[b], (((1,), (1,)), ((), ())), preferred_element_type=f32)
        s = jnp.where(positions < len_ref[b], s, -jnp.inf)
        m = jnp.max(s, axis=1, keepdims=True)
        m_safe = jnp.where(m == -jnp.inf, 0.0, m)
        p = jnp.exp2((s - m_safe) * factor)
        l = jnp.sum(p, axis=1, keepdims=True)
        hi = p.astype(bf16)
        lo = (p - hi.astype(f32)).astype(bf16)
        v_copy(b).wait()
        o2 = jnp.dot(jnp.concatenate([hi, lo], axis=0), v_v[b], preferred_element_type=f32)
        osend[b] = o2[:heads] + o2[heads:]
        obuf[me, b] = osend[b, pl.ds(pl.multiple_of(me * own_heads, 8), own_heads), :]

        def send(k, c):
            p_dev = peer_of(me, k, n_dev)
            pltpu.make_async_remote_copy(
                src_ref=osend.at[b, pl.ds(pl.multiple_of(p_dev * own_heads, 8), own_heads), :],
                dst_ref=obuf.at[me, b], send_sem=o_ssem, recv_sem=o_rsem,
                device_id={"model": p_dev}, device_id_type=pl.DeviceIdType.MESH).start()
            return c
        lax.fori_loop(1, n_dev, send, 0, unroll=True)
        ml = jnp.where(lane == b, m, ml)
        return jnp.where(lane == b + 8, l, ml)

    ml = lax.fori_loop(0, rows, attend, jnp.zeros((heads, LANES), f32))
    mlsend[...] = ml
    own_ml = pl.ds(pl.multiple_of(me * own_heads, 8), own_heads)
    mlbuf[me] = mlsend[own_ml, :]

    def send_ml(k, c):
        p_dev = peer_of(me, k, n_dev)
        pltpu.make_async_remote_copy(
            src_ref=mlsend.at[pl.ds(pl.multiple_of(p_dev * own_heads, 8), own_heads), :],
            dst_ref=mlbuf.at[me], send_sem=ml_ssem, recv_sem=ml_rsem,
            device_id={"model": p_dev}, device_id_type=pl.DeviceIdType.MESH).start()
        return c
    lax.fori_loop(1, n_dev, send_ml, 0, unroll=True)

    wait_bytes(kvbuf.at[pl.ds(0, n_dev - 1)], kv_rsem)
    kv_sum = kvbuf[0]
    for d in range(1, n_dev):
        kv_sum = kv_sum + kvbuf[d]
    kvout_v[...] = kv_sum.astype(bf16)
    k_write = pltpu.make_async_copy(kvout_v.at[0], k_out, out_sem.at[0])
    v_write = pltpu.make_async_copy(kvout_v.at[1], v_out, out_sem.at[1])
    k_write.start()
    v_write.start()
    k_new = kv_sum[0].astype(bf16).astype(f32)
    v_new = kv_sum[1].astype(bf16).astype(f32)

    wait_bytes(mlbuf.at[pl.ds(0, n_dev - 1)], ml_rsem)
    wait_bytes(obuf.at[pl.ds(0, n_dev - 1)], o_rsem)
    for b in range(rows):
        q_own = qbuf[pl.ds(me * own_heads, own_heads), b, :]
        s_new = jnp.sum(q_own * k_new[b:b + 1, :], axis=1, keepdims=True)
        top = s_new
        for d in range(n_dev):
            top = jnp.maximum(top, mlbuf[d, :, b:b + 1])
        w_new = jnp.exp2((s_new - top) * factor)
        total = w_new
        acc = w_new * v_new[b:b + 1, :]
        for d in range(n_dev):
            w_d = jnp.exp2((mlbuf[d, :, b:b + 1] - top) * factor)
            total = total + w_d * mlbuf[d, :, b + 8:b + 9]
            acc = acc + w_d * obuf[d, b]
        astage[b] = acc / total
    for h in range(own_heads):
        a_v[:, h * head_dim:(h + 1) * head_dim] = astage[:, h, :].astype(bf16)

    def y_step(j, c):
        wo_copy(j).wait()
        ysend[j] = jnp.dot(a_v[...], wo_v[j], preferred_element_type=f32)

        @pl.when(j < n_dev - 1)
        def _():
            pltpu.make_async_remote_copy(
                src_ref=ysend.at[j], dst_ref=ybuf.at[me], send_sem=y_ssem, recv_sem=y_rsem,
                device_id={"model": lax.rem(me + 1 + j, n_dev)},
                device_id_type=pl.DeviceIdType.MESH).start()
        return c
    lax.fori_loop(0, n_dev, y_step, 0)
    ybuf[me] = ysend[n_dev - 1]
    wait_bytes(ybuf.at[pl.ds(0, n_dev - 1)], y_rsem)
    y_sum = ybuf[0]
    for d in range(1, n_dev):
        y_sum = y_sum + ybuf[d]
    y_v[:, own_cols(me)] = (x_v[:, own_cols(me)].astype(f32) + y_sum).astype(bf16)
    send_all(y_v.at[:, own_cols(me)], y_v.at[:, own_cols(me)], g_ssem, g_rsem)
    wait_bytes(y_v.at[:, pl.ds(0, (n_dev - 1) * y_cols)], g_rsem)
    y_write = pltpu.make_async_copy(y_v, y_out, out_sem.at[2])
    y_write.start()

    wait_bytes(qbuf.at[pl.ds(0, heads - own_heads)], q_ssem)
    wait_bytes(kvbuf.at[pl.ds(0, n_dev - 1)], kv_ssem)
    wait_bytes(obuf.at[pl.ds(0, n_dev - 1)], o_ssem)
    wait_bytes(mlbuf.at[pl.ds(0, n_dev - 1)], ml_ssem)
    wait_bytes(ybuf.at[pl.ds(0, n_dev - 1)], y_ssem)
    wait_bytes(y_v.at[:, pl.ds(0, (n_dev - 1) * y_cols)], g_ssem)
    k_write.wait()
    v_write.wait()
    y_write.wait()


def solution(mesh):
    n_dev = mesh.shape["model"]

    def local_step(x, w_q, w_k, w_v, w_o, k_cache, v_cache, lengths):
        rows, _, t_local, head_dim = k_cache.shape
        depth = x.shape[1]
        own_heads = w_q.shape[1] // head_dim
        heads = own_heads * n_dev
        y_cols = w_o.shape[1] // n_dev
        kv_rows = depth // n_dev
        f32, bf16 = jnp.float32, jnp.bfloat16
        hbm = pl.BlockSpec(memory_space=pl.ANY)
        dma = pltpu.SemaphoreType.DMA
        return pl.pallas_call(
            functools.partial(kernel, n_dev),
            out_shape=(jax.ShapeDtypeStruct((rows, depth), bf16),
                       jax.ShapeDtypeStruct((rows, head_dim), bf16),
                       jax.ShapeDtypeStruct((rows, head_dim), bf16)),
            in_specs=[hbm] * 7 + [pl.BlockSpec(memory_space=pltpu.SMEM)],
            out_specs=(hbm, hbm, hbm),
            scratch_shapes=[
                pltpu.VMEM((rows, depth), bf16),
                pltpu.VMEM((RING, depth, head_dim), bf16),
                pltpu.VMEM((2, kv_rows, head_dim), bf16),
                pltpu.VMEM((rows, t_local, head_dim), bf16),
                pltpu.VMEM((rows, t_local, head_dim), bf16),
                pltpu.VMEM((n_dev, w_o.shape[0], y_cols), bf16),
                pltpu.VMEM((heads, rows, head_dim), f32),
                pltpu.VMEM((n_dev, 2, rows, head_dim), f32),
                pltpu.VMEM((rows, heads, head_dim), f32),
                pltpu.VMEM((n_dev, rows, own_heads, head_dim), f32),
                pltpu.VMEM((heads, LANES), f32),
                pltpu.VMEM((n_dev, own_heads, LANES), f32),
                pltpu.VMEM((rows, own_heads, head_dim), f32),
                pltpu.VMEM((rows, own_heads * head_dim), bf16),
                pltpu.VMEM((n_dev, rows, y_cols), f32),
                pltpu.VMEM((n_dev, rows, y_cols), f32),
                pltpu.VMEM((rows, depth), bf16),
                pltpu.VMEM((2, rows, head_dim), bf16),
                dma, dma((RING,)), dma((2,)), dma((rows,)), dma((rows,)), dma((n_dev,)), dma((3,)),
            ] + [dma] * 12,
            compiler_params=pltpu.CompilerParams(
                collective_id=0, has_side_effects=True, vmem_limit_bytes=67043328),
        )(x, w_q, w_k, w_v, w_o, k_cache, v_cache, lengths)

    row_spec = P("replica", None)
    cache_spec = P("replica", None, "model", None)
    return jax.shard_map(
        local_step, mesh=mesh,
        in_specs=(row_spec, P(None, "model"), P(), P(), P("model", None), cache_spec, cache_spec, P("replica")),
        out_specs=(row_spec, row_spec, row_spec), check_vma=False)
```

time: 184 us -> 55.8 us (0.30)
  waiting for transfers between devices: 66.6 us -> 0 us
  blocking collectives: 59.7 us -> 0 us
  Pallas kernels: 0 us -> 50.8 us
  matrix products: 39.5 us -> 0 us
  between operations: 14.1 us -> 0.64 us
  local copies, waits for them, and re-layouts: 1.29 us -> 4.09 us
  other arithmetic: 2.39 us -> 0 us
    pallas_call x0 -> x1, Pallas kernels: none -> 50.8 us  [local_step(): pl.pallas_call(functools.partial(kernel, n_dev), out_shape=(jax.ShapeDtyp...]
    psum x1 -> x0, waiting for transfers between devices: 42.7 us -> none  [local_step(): lax.psum(y_part, 'model')]
    dot_general x7 -> x0, matrix products: 39.5 us -> none  [the longest x1 14 us: local_step(): y_part = jnp.dot(attn_local, w_o, preferred_element_type=jnp.float32)]
    reduce_scatter x1 -> x0, waiting for transfers between devices: 23.9 us -> none  [local_step(): lax.psum_scatter(part_out, 'model', scatter_dimension=1, tiled=True)]
    psum x1 -> x0, blocking collectives: 23.1 us -> none  [local_step(): total = lax.psum(jnp.sum(weights, axis=-1), 'model') + weight_new]
    pmax x1 -> x0, blocking collectives: 22.3 us -> none  [local_step(): top = jnp.maximum(lax.pmax(jnp.max(scores, axis=-1), 'model'), score_new)]
    all_gather x1 -> x0, blocking collectives: 14.4 us -> none  [local_step(): q_all = lax.all_gather(q_local, 'model', axis=1, tiled=True)]
    unnamed x10 -> x3, local copies, waits for them, and re-layouts: 1.29 us -> 4.09 us
  transfers between devices with their start and end apart: 2 -> 0, of which waited for: 2 -> 0; matrix products, arithmetic and copies ran while one was open for 2% -> 0% of each run, Pallas kernels for 0% -> 0%
where the time goes in v1:
time: 55.8 us; the launch traced here: 55.6 us
  Pallas kernels  50.8 us (91%)
  local copies, waits for them, and re-layouts  4.09 us (7%)
  between operations  0.64 us (1%)
    pallas_call x1, Pallas kernels, local_step(): pl.pallas_call(functools.partial(kernel, n_dev), out_shape=(jax.ShapeDtyp...  50.8 us
    unnamed x3, local copies, waits for them, and re-layouts  4.09 us

profile of v1, /device:TPU:0, one launch (start us, length us, event | category | flops | bytes accessed | tf_op | source)
XLA Modules:
  0.0 55.6 jit_solution(17515697941880143679)
XLA Ops:
  0.6 50.8 %shard_map.103 = (bf16[6,7168]{1,0:T(8,128)(2,1)}, bf16[6,256]{1,0:T(8,128)(2,1)}, bf16[6,256]{1,0:T(8,128)(2,1)}) custom-call(bf16[6,7168]{1,0:T(8,128)(2,1)} %x_hbm.1, bf16[7168,2048]{1,0:T(8,128)(2,1)} %wq_hbm.1, bf16[7168,256]{1,0:T(8,128)(2,1)} %wk_hbm.1, bf16[7168,256]{1,0:T(8,128)(2,1)} %wv_hbm.1, bf16[2048,7168]{1,0:T(8,128)(2,1)} %wo_hbm.1, ...), custom_call_target="tpu_custom_call" | custom-call | tf_op jit(solution)/shard_map/pallas_call | solution.py:240
  51.5 1.6 %copy.14 = bf16[6,7168]{1,0:T(8,128)(2,1)} copy(bf16[6,7168]{1,0:T(8,128)(2,1)} %get-tuple-element.6) | data formatting | bytes 172032
  53.0 1.3 %copy.15 = bf16[6,256]{1,0:T(8,128)(2,1)} copy(bf16[6,256]{1,0:T(8,128)(2,1)} %get-tuple-element.7) | data formatting | bytes 6144
  54.3 1.3 %copy.16 = bf16[6,256]{1,0:T(8,128)(2,1)} copy(bf16[6,256]{1,0:T(8,128)(2,1)} %get-tuple-element.8) | data formatting | bytes 6144

commit v2 on v1

v2 whole, which is shorter than its diff:
```python
import functools
import math

import jax
import jax.numpy as jnp
from jax import lax
from jax.experimental import pallas as pl
from jax.experimental.pallas import tpu as pltpu
from jax.sharding import PartitionSpec as P

RING = 4
LANES = 128
WIDE = 256
MESH = pl.DeviceIdType.MESH


def kernel(n_dev, x_hbm, wq_hbm, wk_hbm, wv_hbm, wo_hbm, kc_hbm, vc_hbm, len_hbm,
           y_out, k_out, v_out,
           len_s, x_v, w_v, wkv_v, k_v, v_v,
           qbuf, kvbuf, s_buf, osend, obuf, mlsend, mlbuf, astage, a_v, ysend, ybuf, y_v, kvout_v,
           len_sem, x_sem, wq_sem, wkv_sem, k_sem, v_sem, wo_sem, out_sem,
           q_ssem, q_rsem, kv_ssem, kv_rsem, o_ssem, o_rsem, ml_ssem, ml_rsem,
           y_ssem, y_rsem, g_ssem, g_rsem):
    rows, depth = x_hbm.shape
    head_dim = wk_hbm.shape[1]
    own_heads = wq_hbm.shape[1] // head_dim
    t_local = kc_hbm.shape[2]
    heads = own_heads * n_dev
    kv_rows = depth // n_dev
    y_cols = wo_hbm.shape[1] // n_dev
    o_rows = wo_hbm.shape[0]
    chips = n_dev // 2
    pieces = 2 * y_cols // WIDE
    ring_base = w_v.shape[0] - RING * depth
    me = lax.axis_index("model")
    chip, core = lax.div(me, 2), lax.rem(me, 2)
    factor = head_dim ** -0.5 * math.log2(math.e)
    f32, bf16 = jnp.float32, jnp.bfloat16

    def peer(d_chip, d_core):
        c_x = lax.rem(lax.rem(chip, 2) + d_chip % 2, 2)
        c_y = lax.rem(lax.div(chip, 2) + d_chip // 2, 2)
        return (c_y * 2 + c_x) * 2 + lax.rem(core + d_core, 2)

    peers = [peer(dc, dk) for dc, dk in ((3, 0), (3, 1), (1, 0), (2, 0), (1, 1), (2, 1), (0, 1))]

    def cols(i, width):
        return pl.ds(pl.multiple_of(i * width, LANES), width)

    def row_block(i, size):
        return pl.ds(pl.multiple_of(i * size, 8), size)

    def wq_slot(h):
        return pl.ds(pl.multiple_of(ring_base + lax.rem(h, RING) * depth, 256), depth)

    def wq_copy(h):
        return pltpu.make_async_copy(
            wq_hbm.at[:, cols(h, head_dim)], w_v.at[wq_slot(h), :], wq_sem.at[lax.rem(h, RING)])

    def wo_copy(g, i):
        c = lax.rem(chip + 1 + g, chips)
        piece = lax.rem(i + (pieces // 2) * (1 - core), pieces) if g == chips - 1 else i
        return pltpu.make_async_copy(
            wo_hbm.at[:, cols(c * pieces + piece, WIDE)],
            w_v.at[pl.ds((g * pieces + i) * o_rows, o_rows), :], wo_sem.at[g])

    def wait_bytes(ref, sem):
        pltpu.make_async_copy(ref, ref, sem).wait()

    def wait_group(g):
        wait_bytes(w_v.at[pl.ds(g * pieces * o_rows, pieces * o_rows), :], wo_sem.at[g])

    def send(src, dst, ssem, rsem, p):
        pltpu.make_async_remote_copy(
            src_ref=src, dst_ref=dst, send_sem=ssem, recv_sem=rsem,
            device_id={"model": p}, device_id_type=MESH).start()

    def send_all(ref, ssem, rsem):
        for p in peers:
            send(ref, ref, ssem, rsem, p)

    kv_slice = pl.ds(pl.multiple_of(me * kv_rows, LANES), kv_rows)
    x_copy = pltpu.make_async_copy(x_hbm, x_v, x_sem)
    len_copy = pltpu.make_async_copy(len_hbm, len_s, len_sem)
    wk_copy = pltpu.make_async_copy(wk_hbm.at[kv_slice, :], wkv_v.at[0], wkv_sem.at[0])
    wv_copy = pltpu.make_async_copy(wv_hbm.at[kv_slice, :], wkv_v.at[1], wkv_sem.at[1])
    k_copy = [pltpu.make_async_copy(kc_hbm.at[b, 0], k_v.at[b], k_sem.at[b]) for b in range(rows)]
    v_copy = [pltpu.make_async_copy(vc_hbm.at[b, 0], v_v.at[b], v_sem.at[b]) for b in range(rows)]

    x_copy.start()
    wq_copy(0).start()
    barrier = pltpu.get_barrier_semaphore()
    for p in peers:
        pl.semaphore_signal(barrier, inc=1, device_id={"model": p}, device_id_type=MESH)
    for h in range(1, RING):
        wq_copy(h).start()
    len_copy.start()
    with jax.named_scope('x_wait'):
        x_copy.wait()

    def q_step(h, c):
        with jax.named_scope('q_wait'):
            wq_copy(h).wait()
        q = jnp.dot(x_v[...], w_v[wq_slot(h), :], preferred_element_type=f32)
        block = me * own_heads + h
        qbuf[block] = q.astype(bf16).astype(f32)

        @pl.when(h == 0)
        def _():
            with jax.named_scope('barrier'):
                pl.semaphore_wait(barrier, n_dev - 1)

        send_all(qbuf.at[block], q_ssem, q_rsem)

        @pl.when(h < own_heads - RING)
        def _():
            wq_copy(h + RING).start()

        @pl.when(h == own_heads - RING)
        def _():
            wk_copy.start()
            wv_copy.start()
            for c in k_copy:
                c.start()

        @pl.when(h == own_heads - RING + 1)
        def _():
            for c in v_copy:
                c.start()

        @pl.when(h == own_heads - RING + 2)
        def _():
            for g in range(2):
                for i in range(pieces):
                    wo_copy(g, i).start()
        return c

    lax.fori_loop(0, own_heads, q_step, 0)
    for g in range(2, chips):
        for i in range(pieces):
            wo_copy(g, i).start()

    with jax.named_scope('wkv_wait'):
        wk_copy.wait()
        wv_copy.wait()
    x_part = x_v[:, kv_slice]
    for i in range(2):
        kvbuf[me, i] = jnp.dot(x_part, wkv_v[i], preferred_element_type=f32)
    send_all(kvbuf.at[me], kv_ssem, kv_rsem)

    with jax.named_scope('k_wait'):
        len_copy.wait()
        for c in k_copy:
            c.wait()
    with jax.named_scope('q_recv'):
        wait_bytes(qbuf.at[pl.ds(0, heads - own_heads)], q_rsem)

    positions = me * t_local + lax.broadcasted_iota(jnp.int32, (1, t_local), 1)
    lane = lax.broadcasted_iota(jnp.int32, (heads, LANES), 1)

    def scores(b):
        q_b = qbuf[:, b, :].astype(bf16)
        s_buf[b % 2] = lax.dot_general(q_b, k_v[b], (((1,), (1,)), ((), ())), preferred_element_type=f32)

    ml = jnp.zeros((heads, LANES), f32)
    scores(0)
    with jax.named_scope('v_wait'):
        for c in v_copy:
            c.wait()
    for b in range(rows):
        if b + 1 < rows:
            scores(b + 1)
        s = jnp.where(positions < len_s[b], s_buf[b % 2], -jnp.inf)
        m = jnp.max(s, axis=1, keepdims=True)
        m_safe = jnp.where(m == -jnp.inf, 0.0, m)
        p = jnp.exp2((s - m_safe) * factor)
        l = jnp.sum(p, axis=1, keepdims=True)
        hi = p.astype(bf16)
        lo = (p - hi.astype(f32)).astype(bf16)
        o2 = jnp.dot(jnp.concatenate([hi, lo], axis=0), v_v[b], preferred_element_type=f32)
        osend[b] = o2[:heads] + o2[heads:]
        obuf[me, b] = osend[b, row_block(me, own_heads), :]
        for d in peers:
            send(osend.at[b, row_block(d, own_heads), :], obuf.at[me, b], o_ssem, o_rsem, d)
        ml = jnp.where(lane == b, m, ml)
        ml = jnp.where(lane == b + 8, l, ml)
    mlsend[...] = ml
    mlbuf[me] = mlsend[row_block(me, own_heads), :]
    for d in peers:
        send(mlsend.at[row_block(d, own_heads), :], mlbuf.at[me], ml_ssem, ml_rsem, d)

    with jax.named_scope('kv_recv'):
        wait_bytes(kvbuf.at[pl.ds(0, n_dev - 1)], kv_rsem)
    kv_sum = kvbuf[0]
    for d in range(1, n_dev):
        kv_sum = kv_sum + kvbuf[d]
    kvout_v[...] = kv_sum.astype(bf16)
    k_write = pltpu.make_async_copy(kvout_v.at[0], k_out, out_sem.at[0])
    v_write = pltpu.make_async_copy(kvout_v.at[1], v_out, out_sem.at[1])
    k_write.start()
    v_write.start()
    k_new = kv_sum[0].astype(bf16).astype(f32)
    v_new = kv_sum[1].astype(bf16).astype(f32)

    with jax.named_scope('ml_recv'):
        wait_bytes(mlbuf.at[pl.ds(0, n_dev - 1)], ml_rsem)
    with jax.named_scope('o_recv'):
        wait_bytes(obuf.at[pl.ds(0, n_dev - 1)], o_rsem)
    for b in range(rows):
        q_own = qbuf[pl.ds(me * own_heads, own_heads), b, :]
        s_new = jnp.sum(q_own * k_new[b:b + 1, :], axis=1, keepdims=True)
        top = s_new
        for d in range(n_dev):
            top = jnp.maximum(top, mlbuf[d, :, b:b + 1])
        w_new = jnp.exp2((s_new - top) * factor)
        total = w_new
        acc = w_new * v_new[b:b + 1, :]
        for d in range(n_dev):
            w_d = jnp.exp2((mlbuf[d, :, b:b + 1] - top) * factor)
            total = total + w_d * mlbuf[d, :, b + 8:b + 9]
            acc = acc + w_d * obuf[d, b]
        astage[b] = acc / total
    for h in range(own_heads):
        a_v[:, h * head_dim:(h + 1) * head_dim] = astage[:, h, :].astype(bf16)

    def half(h):
        return pl.ds(pl.multiple_of(h * y_cols, LANES), y_cols)

    def y_piece(g, i, col):
        ysend[g, :, cols(col, WIDE)] = jnp.dot(
            a_v[...], w_v[pl.ds(pl.multiple_of((g * pieces + i) * o_rows, 256), o_rows), :],
            preferred_element_type=f32)

    def y_group(g, c):
        with jax.named_scope('wo_wait'):
            wait_group(g)
        target = 2 * lax.rem(chip + 1 + g, chips)
        for i in range(pieces):
            y_piece(g, i, i)
            if i == pieces // 2:
                send(ysend.at[g, :, half(0)], ybuf.at[me], y_ssem, y_rsem, target)
        send(ysend.at[g, :, half(1)], ybuf.at[me], y_ssem, y_rsem, target + 1)
        return c

    lax.fori_loop(0, chips - 1, y_group, 0)
    last = chips - 1
    with jax.named_scope('wo_wait'):
        wait_group(last)
    for i in range(pieces):
        y_piece(last, i, lax.rem(i + (pieces // 2) * (1 - core), pieces))
        if i == pieces // 2:
            send(ysend.at[last, :, half(1 - core)], ybuf.at[me], y_ssem, y_rsem, peers[-1])
    ybuf[me] = ysend[last, :, half(core)]
    with jax.named_scope('y_recv'):
        wait_bytes(ybuf.at[pl.ds(0, n_dev - 1)], y_rsem)
    y_sum = ybuf[0]
    for d in range(1, n_dev):
        y_sum = y_sum + ybuf[d]
    y_v[:, half(me)] = (x_v[:, half(me)].astype(f32) + y_sum).astype(bf16)
    send_all(y_v.at[:, half(me)], g_ssem, g_rsem)
    with jax.named_scope('g_recv'):
        wait_bytes(y_v.at[:, pl.ds(0, (n_dev - 1) * y_cols)], g_rsem)
    y_write = pltpu.make_async_copy(y_v, y_out, out_sem.at[2])
    y_write.start()

    wait_bytes(qbuf.at[pl.ds(0, heads - own_heads)], q_ssem)
    wait_bytes(kvbuf.at[pl.ds(0, n_dev - 1)], kv_ssem)
    wait_bytes(obuf.at[pl.ds(0, n_dev - 1)], o_ssem)
    wait_bytes(mlbuf.at[pl.ds(0, n_dev - 1)], ml_ssem)
    wait_bytes(ybuf.at[pl.ds(0, n_dev - 1)], y_ssem)
    wait_bytes(y_v.at[:, pl.ds(0, (n_dev - 1) * y_cols)], g_ssem)
    with jax.named_scope('out_wait'):
        k_write.wait()
        v_write.wait()
        y_write.wait()


def solution(mesh):
    n_dev = mesh.shape["model"]

    def local_step(x, w_q, w_k, w_v, w_o, k_cache, v_cache, lengths):
        rows, _, t_local, head_dim = k_cache.shape
        depth = x.shape[1]
        own_heads = w_q.shape[1] // head_dim
        heads = own_heads * n_dev
        y_cols = w_o.shape[1] // n_dev
        chips = n_dev // 2
        f32, bf16 = jnp.float32, jnp.bfloat16
        hbm = pl.BlockSpec(memory_space=pl.ANY)
        dma = pltpu.SemaphoreType.DMA
        return pl.pallas_call(
            functools.partial(kernel, n_dev),
            out_shape=(jax.ShapeDtypeStruct((rows, depth), bf16),
                       jax.ShapeDtypeStruct((rows, head_dim), bf16),
                       jax.ShapeDtypeStruct((rows, head_dim), bf16)),
            in_specs=[hbm] * 8,
            out_specs=(hbm, hbm, hbm),
            scratch_shapes=[
                pltpu.SMEM((rows,), jnp.int32),
                pltpu.VMEM((rows, depth), bf16),
                pltpu.VMEM((w_o.shape[0] * w_o.shape[1] // WIDE, WIDE), bf16),
                pltpu.VMEM((2, depth // n_dev, head_dim), bf16),
                pltpu.VMEM((rows, t_local, head_dim), bf16),
                pltpu.VMEM((rows, t_local, head_dim), bf16),
                pltpu.VMEM((heads, rows, head_dim), f32),
                pltpu.VMEM((n_dev, 2, rows, head_dim), f32),
                pltpu.VMEM((2, heads, t_local), f32),
                pltpu.VMEM((rows, heads, head_dim), f32),
                pltpu.VMEM((n_dev, rows, own_heads, head_dim), f32),
                pltpu.VMEM((heads, LANES), f32),
                pltpu.VMEM((n_dev, own_heads, LANES), f32),
                pltpu.VMEM((rows, own_heads, head_dim), f32),
                pltpu.VMEM((rows, own_heads * head_dim), bf16),
                pltpu.VMEM((chips, rows, 2 * y_cols), f32),
                pltpu.VMEM((n_dev, rows, y_cols), f32),
                pltpu.VMEM((rows, depth), bf16),
                pltpu.VMEM((2, rows, head_dim), bf16),
                dma, dma, dma((RING,)), dma((2,)), dma((rows,)), dma((rows,)), dma((chips,)), dma((3,)),
            ] + [dma] * 12,
            compiler_params=pltpu.CompilerParams(
                collective_id=0, has_side_effects=True, vmem_limit_bytes=67043328),
        )(x, w_q, w_k, w_v, w_o, k_cache, v_cache, lengths)

    row_spec = P("replica", None)
    cache_spec = P("replica", None, "model", None)
    return jax.shard_map(
        local_step, mesh=mesh,
        in_specs=(row_spec, P(None, "model"), P(), P(), P("model", None), cache_spec, cache_spec, P("replica")),
        out_specs=(row_spec, row_spec, row_spec), check_vma=False)
```

time: 55.8 us -> 41.1 us (0.74)
  Pallas kernels: 50.8 us -> 36.2 us
    pallas_call x1, Pallas kernels: 50.8 us -> 36.2 us  [local_step(): pl.pallas_call(functools.partial(kernel, n_dev), out_shape=(jax.ShapeDtyp...]
where the time goes in v2:
time: 41.1 us; the launch traced here: 41 us
  Pallas kernels  36.2 us (88%)
  local copies, waits for them, and re-layouts  4.09 us (10%)
  between operations  0.64 us (2%)
    pallas_call x1, Pallas kernels, local_step(): pl.pallas_call(functools.partial(kernel, n_dev), out_shape=(jax.ShapeDtyp...  36.2 us
    unnamed x3, local copies, waits for them, and re-layouts  4.09 us

profile of v2, /device:TPU:0, one launch (start us, length us, event | category | flops | bytes accessed | tf_op | source)
XLA Modules:
  0.0 41.0 jit_solution(2061071810478258219)
XLA Ops:
  0.6 36.2 %shard_map.103 = (bf16[6,7168]{1,0:T(8,128)(2,1)}, bf16[6,256]{1,0:T(8,128)(2,1)}, bf16[6,256]{1,0:T(8,128)(2,1)}) custom-call(bf16[6,7168]{1,0:T(8,128)(2,1)} %x_hbm.1, bf16[7168,2048]{1,0:T(8,128)(2,1)} %wq_hbm.1, bf16[7168,256]{1,0:T(8,128)(2,1)} %wk_hbm.1, bf16[7168,256]{1,0:T(8,128)(2,1)} %wv_hbm.1, bf16[2048,7168]{1,0:T(8,128)(2,1)} %wo_hbm.1, ...), custom_call_target="tpu_custom_call" | custom-call | tf_op jit(solution)/shard_map/pallas_call | solution.py:291
  36.9 1.6 %copy.14 = bf16[6,7168]{1,0:T(8,128)(2,1)} copy(bf16[6,7168]{1,0:T(8,128)(2,1)} %get-tuple-element.6) | data formatting | bytes 172032
  38.4 1.3 %copy.15 = bf16[6,256]{1,0:T(8,128)(2,1)} copy(bf16[6,256]{1,0:T(8,128)(2,1)} %get-tuple-element.7) | data formatting | bytes 6144
  39.7 1.3 %copy.16 = bf16[6,256]{1,0:T(8,128)(2,1)} copy(bf16[6,256]{1,0:T(8,128)(2,1)} %get-tuple-element.8) | data formatting | bytes 6144

commit v3 on v2

--- a/solution.py
+++ b/solution.py
@@ -17,8 +17,8 @@
 def kernel(n_dev, x_hbm, wq_hbm, wk_hbm, wv_hbm, wo_hbm, kc_hbm, vc_hbm, len_hbm,
            y_out, k_out, v_out,
            len_s, x_v, w_v, wkv_v, k_v, v_v,
-           qbuf, kvbuf, s_buf, osend, obuf, mlsend, mlbuf, astage, a_v, ysend, ybuf, y_v, kvout_v,
-           len_sem, x_sem, wq_sem, wkv_sem, k_sem, v_sem, wo_sem, out_sem,
+           qbuf, kvbuf, s_buf, osend, obuf, mlsend, mlbuf, astage, a_v, ysend, ybuf, y_v,
+           len_sem, x_sem, wq_sem, wkv_sem, k_sem, v_sem, wo_sem,
            q_ssem, q_rsem, kv_ssem, kv_rsem, o_ssem, o_rsem, ml_ssem, ml_rsem,
            y_ssem, y_rsem, g_ssem, g_rsem):
     rows, depth = x_hbm.shape
@@ -194,11 +194,8 @@
     kv_sum = kvbuf[0]
     for d in range(1, n_dev):
         kv_sum = kv_sum + kvbuf[d]
-    kvout_v[...] = kv_sum.astype(bf16)
-    k_write = pltpu.make_async_copy(kvout_v.at[0], k_out, out_sem.at[0])
-    v_write = pltpu.make_async_copy(kvout_v.at[1], v_out, out_sem.at[1])
-    k_write.start()
-    v_write.start()
+    k_out[...] = kv_sum[0].astype(bf16)
+    v_out[...] = kv_sum[1].astype(bf16)
     k_new = kv_sum[0].astype(bf16).astype(f32)
     v_new = kv_sum[1].astype(bf16).astype(f32)
 
@@ -260,8 +257,7 @@
     send_all(y_v.at[:, half(me)], g_ssem, g_rsem)
     with jax.named_scope('g_recv'):
         wait_bytes(y_v.at[:, pl.ds(0, (n_dev - 1) * y_cols)], g_rsem)
-    y_write = pltpu.make_async_copy(y_v, y_out, out_sem.at[2])
-    y_write.start()
+    y_out[...] = y_v[...]
 
     wait_bytes(qbuf.at[pl.ds(0, heads - own_heads)], q_ssem)
     wait_bytes(kvbuf.at[pl.ds(0, n_dev - 1)], kv_ssem)
@@ -269,10 +265,15 @@
     wait_bytes(mlbuf.at[pl.ds(0, n_dev - 1)], ml_ssem)
     wait_bytes(ybuf.at[pl.ds(0, n_dev - 1)], y_ssem)
     wait_bytes(y_v.at[:, pl.ds(0, (n_dev - 1) * y_cols)], g_ssem)
-    with jax.named_scope('out_wait'):
-        k_write.wait()
-        v_write.wait()
-        y_write.wait()
+
+
+def store_kernel(*refs):
+    sems, n_out = refs[-1], len(refs) // 2
+    copies = [pltpu.make_async_copy(refs[i], refs[n_out + i], sems.at[i]) for i in range(n_out)]
+    for c in copies:
+        c.start()
+    for c in copies:
+        c.wait()
 
 
 def solution(mesh):
@@ -288,13 +289,14 @@
         f32, bf16 = jnp.float32, jnp.bfloat16
         hbm = pl.BlockSpec(memory_space=pl.ANY)
         dma = pltpu.SemaphoreType.DMA
-        return pl.pallas_call(
+        vm = pl.BlockSpec(memory_space=pltpu.VMEM)
+        y, k_new, v_new = pl.pallas_call(
             functools.partial(kernel, n_dev),
-            out_shape=(jax.ShapeDtypeStruct((rows, depth), bf16),
-                       jax.ShapeDtypeStruct((rows, head_dim), bf16),
-                       jax.ShapeDtypeStruct((rows, head_dim), bf16)),
+            out_shape=(pltpu.VMEM((rows, depth), bf16),
+                       pltpu.VMEM((rows, head_dim), bf16),
+                       pltpu.VMEM((rows, head_dim), bf16)),
             in_specs=[hbm] * 8,
-            out_specs=(hbm, hbm, hbm),
+            out_specs=(vm, vm, vm),
             scratch_shapes=[
                 pltpu.SMEM((rows,), jnp.int32),
                 pltpu.VMEM((rows, depth), bf16),
@@ -314,12 +316,20 @@
                 pltpu.VMEM((chips, rows, 2 * y_cols), f32),
                 pltpu.VMEM((n_dev, rows, y_cols), f32),
                 pltpu.VMEM((rows, depth), bf16),
-                pltpu.VMEM((2, rows, head_dim), bf16),
-                dma, dma, dma((RING,)), dma((2,)), dma((rows,)), dma((rows,)), dma((chips,)), dma((3,)),
+                dma, dma, dma((RING,)), dma((2,)), dma((rows,)), dma((rows,)), dma((chips,)),
             ] + [dma] * 12,
             compiler_params=pltpu.CompilerParams(
-                collective_id=0, has_side_effects=True, vmem_limit_bytes=67043328),
+                collective_id=0, has_side_effects=True, vmem_limit_bytes=63000000),
         )(x, w_q, w_k, w_v, w_o, k_cache, v_cache, lengths)
+        outs = (y, k_new, v_new)
+        return pl.pallas_call(
+            store_kernel,
+            out_shape=tuple(jax.ShapeDtypeStruct(o.shape, o.dtype) for o in outs),
+            in_specs=[hbm] * 3,
+            out_specs=(hbm,) * 3,
+            scratch_shapes=[dma((len(outs),))],
+            compiler_params=pltpu.CompilerParams(vmem_limit_bytes=1 << 20),
+        )(*outs)
 
     row_spec = P("replica", None)
     cache_spec = P("replica", None, "model", None)

time: 41.1 us -> 37 us (0.900)
  local copies, waits for them, and re-layouts: 4.09 us -> 0 us
    unnamed x3 -> x0, local copies, waits for them, and re-layouts: 4.09 us -> none
    pallas_call x1 -> x2, Pallas kernels: 36.2 us -> 36.3 us  [the longest x1 35.6 us: local_step(): pl.pallas_call(functools.partial(kernel, n_dev), out_shape=(pltpu.VMEM((r...]
where the time goes in v3:
time: 37 us; the launch traced here: 36.9 us
  Pallas kernels  36.3 us (98%)
  between operations  0.64 us (2%)
    pallas_call x1, Pallas kernels, local_step(): pl.pallas_call(functools.partial(kernel, n_dev), out_shape=(pltpu.VMEM((r...  35.6 us

profile of v3, /device:TPU:0, one launch (start us, length us, event | category | flops | bytes accessed | tf_op | source)
XLA Modules:
  0.0 36.9 jit_solution(16246511199989564196)
XLA Ops:
  0.6 35.6 %shard_map.103 = (bf16[6,7168]{1,0:T(8,128)(2,1)S(1)}, bf16[6,256]{1,0:T(8,128)(2,1)S(1)}, bf16[6,256]{1,0:T(8,128)(2,1)S(1)}) custom-call(bf16[6,7168]{1,0:T(8,128)(2,1)} %x_hbm.1, bf16[7168,2048]{1,0:T(8,128)(2,1)} %wq_hbm.1, bf16[7168,256]{1,0:T(8,128)(2,1)} %wk_hbm.1, bf16[7168,256]{1,0:T(8,128)(2,1)} %wv_hbm.1, bf16[2048,7168]{1,0:T(8,128)(2,1)} %wo_hbm.1, ...), custom_call_target="tpu_custom_call" | custom-call | tf_op jit(solution)/shard_map/pallas_call | solution.py:293
  36.2 0.7 %shard_map.104 = (bf16[6,7168]{1,0:T(8,128)(2,1)}, bf16[6,256]{1,0:T(8,128)(2,1)}, bf16[6,256]{1,0:T(8,128)(2,1)}) custom-call(bf16[6,7168]{1,0:T(8,128)(2,1)S(1)} %get-tuple-element.6.refs_0_, bf16[6,256]{1,0:T(8,128)(2,1)S(1)} %get-tuple-element.7.refs_1_, bf16[6,256]{1,0:T(8,128)(2,1)S(1)} %get-tuple-element.8.refs_2_), custom_call_target="tpu_custom_call" | custom-call | tf_op jit(solution)/shard_map/pallas_call | solution.py:325

commit v4 on v3

v4 whole, which is shorter than its diff:
```python
import functools
import math

import jax
import jax.numpy as jnp
from jax import lax
from jax.experimental import pallas as pl
from jax.experimental.pallas import tpu as pltpu
from jax.sharding import PartitionSpec as P

RING = 4
LANES = 128
WIDE = 256
FIRST = 5
BATCH = 3
SENDS = (3, 2)
MESH = pl.DeviceIdType.MESH


def kernel(n_dev, x_hbm, wq_hbm, wk_hbm, wv_hbm, wo_hbm, kc_hbm, vc_hbm, len_hbm,
           y_out, k_out, v_out,
           len_s, x_v, w_v, wkv_v, k_v, v_v, kvbuf, s_buf, yacc, ysend, ybuf, y_v, *rest):
    part_refs, sems = (rest[:9], rest[9:18]), rest[18:]
    (len_sem, x_sem, wq_sem, wkv_sem, k_sem, v_sem, wo_sem,
     kv_ssem, kv_rsem, y_ssem, y_rsem, g_ssem, g_rsem, q_ssem, q_rsem, o_ssem, o_rsem, ml_ssem, ml_rsem) = sems
    rows, depth = x_hbm.shape
    head_dim = wk_hbm.shape[1]
    own_heads = wq_hbm.shape[1] // head_dim
    t_local = kc_hbm.shape[2]
    kv_rows = depth // n_dev
    y_cols = wo_hbm.shape[1] // n_dev
    o_rows = wo_hbm.shape[0]
    chips = n_dev // 2
    pieces = 2 * y_cols // WIDE
    ring_base = w_v.shape[0] - RING * depth
    part_heads = (FIRST, own_heads - FIRST)
    part_row0 = (0, FIRST * head_dim)
    me = lax.axis_index("model")
    chip, core = lax.div(me, 2), lax.rem(me, 2)
    factor = head_dim ** -0.5 * math.log2(math.e)
    f32, bf16 = jnp.float32, jnp.bfloat16

    def chip_at(delta):
        c_x = lax.rem(lax.rem(chip, 2) + delta % 2, 2)
        c_y = lax.rem(lax.div(chip, 2) + delta // 2, 2)
        return c_y * 2 + c_x

    def peer(d_chip, d_core):
        return chip_at(d_chip) * 2 + lax.rem(core + d_core, 2)

    peers = [peer(dc, dk) for dc, dk in ((3, 0), (3, 1), (1, 0), (2, 0), (1, 1), (2, 1), (0, 1))]
    group_chip = [chip_at(d) for d in (3, 1, 2, 0)]

    def cols(i, width):
        return pl.ds(pl.multiple_of(i * width, LANES), width)

    def wq_slot(h):
        return pl.ds(pl.multiple_of(ring_base + lax.rem(h, RING) * depth, 256), depth)

    def wq_copy(h):
        return pltpu.make_async_copy(
            wq_hbm.at[:, cols(h, head_dim)], w_v.at[wq_slot(h), :], wq_sem.at[lax.rem(h, RING)])

    def wo_copy(part, g, i):
        size = part_heads[part] * head_dim
        return pltpu.make_async_copy(
            wo_hbm.at[pl.ds(part_row0[part], size), cols(group_chip[g] * pieces + i, WIDE)],
            w_v.at[pl.ds((g * pieces + i) * o_rows + part_row0[part], size), :], wo_sem.at[part, g])

    def wait_bytes(ref, sem):
        pltpu.make_async_copy(ref, ref, sem).wait()

    def wait_group(part, g):
        wait_bytes(w_v.at[pl.ds(0, pieces * part_heads[part] * head_dim), :], wo_sem.at[part, g])

    def send(src, dst, ssem, rsem, p):
        pltpu.make_async_remote_copy(
            src_ref=src, dst_ref=dst, send_sem=ssem, recv_sem=rsem,
            device_id={"model": p}, device_id_type=MESH).start()

    def send_all(ref, ssem, rsem):
        for p in peers:
            send(ref, ref, ssem, rsem, p)

    kv_slice = pl.ds(pl.multiple_of(me * kv_rows, LANES), kv_rows)
    x_copy = pltpu.make_async_copy(x_hbm, x_v, x_sem)
    len_copy = pltpu.make_async_copy(len_hbm, len_s, len_sem)
    wk_copy = pltpu.make_async_copy(wk_hbm.at[kv_slice, :], wkv_v.at[0], wkv_sem.at[0])
    wv_copy = pltpu.make_async_copy(wv_hbm.at[kv_slice, :], wkv_v.at[1], wkv_sem.at[1])

    def k_copy(b):
        return pltpu.make_async_copy(kc_hbm.at[b, 0], k_v.at[b], k_sem.at[b])

    def v_copy(b):
        return pltpu.make_async_copy(vc_hbm.at[b, 0], v_v.at[b], v_sem.at[b])

    x_copy.start()
    wq_copy(0).start()
    barrier = pltpu.get_barrier_semaphore()
    for p in peers:
        pl.semaphore_signal(barrier, inc=1, device_id={"model": p}, device_id_type=MESH)
    for h in range(1, RING):
        wq_copy(h).start()
    len_copy.start()
    with jax.named_scope('x_wait'):
        x_copy.wait()

    def q_loop(part):
        q_buf, n_heads = part_refs[part][0], part_heads[part]
        h0 = 0 if part == 0 else FIRST

        def q_step(h, c):
            with jax.named_scope('q_wait'):
                wq_copy(h).wait()
            q = jnp.dot(x_v[...], w_v[wq_slot(h), :], preferred_element_type=f32)
            block = me * n_heads + h - h0
            q_buf[block] = q.astype(bf16).astype(f32)
            if part == 0:
                @pl.when(h == 0)
                def _():
                    with jax.named_scope('barrier'):
                        pl.semaphore_wait(barrier, n_dev - 1)

            send_all(q_buf.at[block], q_ssem.at[part], q_rsem.at[part])
            if h0 < own_heads - RING:
                @pl.when(h < own_heads - RING)
                def _():
                    wq_copy(h + RING).start()

            if h0 <= own_heads - RING < h0 + n_heads:
                @pl.when(h == own_heads - RING)
                def _():
                    wk_copy.start()
                    wv_copy.start()

            if h0 <= own_heads - RING + 1 < h0 + n_heads:
                @pl.when(h == own_heads - RING + 1)
                def _():
                    def start_kv(b, c):
                        k_copy(b).start()
                        v_copy(b).start()
                        return c
                    lax.fori_loop(0, rows, start_kv, 0)
            return c

        lax.fori_loop(h0, h0 + n_heads, q_step, 0)

    q_loop(0)
    q_loop(1)
    for part in range(2):
        for g in range(chips):
            for i in range(pieces):
                wo_copy(part, g, i).start()

    positions = me * t_local + lax.broadcasted_iota(jnp.int32, (1, t_local), 1)

    def part_rows(part, b):
        n = (b % SENDS[part]) * part_heads[part]
        return slice(n, n + part_heads[part])

    def attention(part):
        q_buf, o_flat, osend, obuf, mlflat, mlsend, mlbuf = part_refs[part][:7]
        n_heads = part_heads[part]
        n_rows = n_heads * n_dev
        batch = SENDS[part]
        lane = lax.broadcasted_iota(jnp.int32, (n_rows, LANES), 1)

        def scores(b):
            q_b = q_buf[:, b, :].astype(bf16)
            s_buf[b % 3, 0:n_rows] = lax.dot_general(
                q_b, k_v[b], (((1,), (1,)), ((), ())), preferred_element_type=f32)

        def wait_kv(b0):
            with jax.named_scope('kv_wait'):
                for b in range(b0, b0 + BATCH):
                    k_copy(b).wait()
                    v_copy(b).wait()

        with jax.named_scope('q_recv'):
            wait_bytes(q_buf.at[pl.ds(0, n_rows - n_heads)], q_rsem.at[part])
        if part == 0:
            len_copy.wait()
            wait_kv(0)
        m_all = jnp.zeros((n_rows, LANES), f32)
        l_all = jnp.zeros((n_rows, LANES), f32)
        scores(0)
        for b in range(rows):
            if b + 1 < rows:
                if part == 0 and (b + 1) % BATCH == 0:
                    wait_kv(b + 1)
                scores(b + 1)
            s = jnp.where(positions < len_s[b], s_buf[b % 3, 0:n_rows], -jnp.inf)
            m = jnp.max(s, axis=1, keepdims=True)
            m_safe = jnp.where(m == -jnp.inf, 0.0, m)
            p = jnp.exp2((s - m_safe) * factor)
            l = jnp.sum(p, axis=1, keepdims=True)
            hi = p.astype(bf16).astype(f32)
            terms = jnp.concatenate([hi, p - hi], axis=0).astype(bf16)
            o2 = jnp.dot(terms, v_v[b], preferred_element_type=f32)
            o_flat[b] = o2[:n_rows] + o2[n_rows:]
            m_all = jnp.where(lane == b, m, m_all)
            l_all = jnp.where(lane == b, l, l_all)
            for d in range(n_dev):
                osend[b // batch, d, part_rows(part, b), :] = o_flat[b, d * n_heads:(d + 1) * n_heads, :]
            if (b + 1) % batch == 0:
                n = b // batch
                obuf[me, n] = osend[n, me]
                for d in peers:
                    send(osend.at[n, d], obuf.at[me, n], o_ssem.at[part], o_rsem.at[part], d)
        mlflat[0] = m_all
        mlflat[1] = l_all
        for d in range(n_dev):
            mlsend[d] = mlflat[:, d * n_heads:(d + 1) * n_heads, :]
        mlbuf[me] = mlsend[me]
        for d in peers:
            send(mlsend.at[d], mlbuf.at[me], ml_ssem.at[part], ml_rsem.at[part], d)

    with jax.named_scope('wkv_wait'):
        wk_copy.wait()
        wv_copy.wait()
    x_part = x_v[:, kv_slice]
    for i in range(2):
        kvbuf[me, i] = jnp.dot(x_part, wkv_v[i], preferred_element_type=f32)
    send_all(kvbuf.at[me], kv_ssem, kv_rsem)
    attention(0)
    attention(1)

    with jax.named_scope('kv_recv'):
        wait_bytes(kvbuf.at[pl.ds(0, n_dev - 1)], kv_rsem)
    kv_sum = kvbuf[0]
    for d in range(1, n_dev):
        kv_sum = kv_sum + kvbuf[d]
    k_out[...] = kv_sum[0].astype(bf16)
    v_out[...] = kv_sum[1].astype(bf16)
    k_new = kv_sum[0].astype(bf16).astype(f32)
    v_new = kv_sum[1].astype(bf16).astype(f32)

    def combine(part):
        q_buf, _, _, obuf, _, _, mlbuf, a_v, astage = part_refs[part]
        n_heads = part_heads[part]
        lane = lax.broadcasted_iota(jnp.int32, (n_heads, LANES), 1)
        with jax.named_scope('o_recv'):
            wait_bytes(mlbuf.at[pl.ds(0, n_dev - 1)], ml_rsem.at[part])
            wait_bytes(obuf.at[pl.ds(0, n_dev - 1)], o_rsem.at[part])
        s_new = jnp.zeros((n_heads, LANES), f32)
        for b in range(rows):
            q_own = q_buf[pl.ds(me * n_heads, n_heads), b, :]
            s_new = jnp.where(lane == b, jnp.sum(q_own * k_new[b:b + 1, :], axis=1, keepdims=True), s_new)
        top = s_new
        for d in range(n_dev):
            top = jnp.maximum(top, mlbuf[d, 0])
        w_new = jnp.exp2((s_new - top) * factor)
        w = [jnp.exp2((mlbuf[d, 0] - top) * factor) for d in range(n_dev)]
        total = w_new
        for d in range(n_dev):
            total = total + w[d] * mlbuf[d, 1]
        inv = 1.0 / total
        w_new = w_new * inv
        w = [w_d * inv for w_d in w]
        for b in range(rows):
            acc = w_new[:, b:b + 1] * v_new[b:b + 1, :]
            for d in range(n_dev):
                acc = acc + w[d][:, b:b + 1] * obuf[d, b // SENDS[part], part_rows(part, b), :]
            astage[b] = acc
        for h in range(n_heads):
            a_v[:, h * head_dim:(h + 1) * head_dim] = astage[:, h, :].astype(bf16)

    y_blocks = y_cols // LANES

    def y_rows_at(block):
        return slice(block * rows, (block + 1) * rows)

    def y_rows(part, g):
        a_v = part_refs[part][7]
        size = part_heads[part] * head_dim
        for i in range(pieces):
            row = pl.multiple_of((g * pieces + i) * o_rows + part_row0[part], 256)
            y = jnp.dot(a_v[...], w_v[pl.ds(row, size), :], preferred_element_type=f32)
            at = slice(i * WIDE, (i + 1) * WIDE)
            if part == 0:
                yacc[g, :, at] = y
                continue
            y = yacc[g, :, at] + y
            for j in range(WIDE // LANES):
                block = i * (WIDE // LANES) + j
                ysend[g, block // y_blocks, y_rows_at(block % y_blocks), :] = y[:, j * LANES:(j + 1) * LANES]

    def half(h):
        return pl.ds(pl.multiple_of(h * y_cols, LANES), y_cols)

    combine(0)

    def y_first(g, c):
        with jax.named_scope('wo_wait'):
            wait_group(0, g)
        y_rows(0, g)
        return c

    lax.fori_loop(0, chips, y_first, 0)
    combine(1)
    last = chips - 1
    for g in range(chips):
        with jax.named_scope('wo_wait'):
            wait_group(1, g)
        y_rows(1, g)
        if g < last:
            for k in range(2):
                send(ysend.at[g, k], ybuf.at[me], y_ssem, y_rsem, 2 * group_chip[g] + k)
    send(ysend.at[last, 1 - core], ybuf.at[me], y_ssem, y_rsem, peers[-1])
    ybuf[me] = ysend[last, core]
    with jax.named_scope('y_recv'):
        wait_bytes(ybuf.at[pl.ds(0, n_dev - 1)], y_rsem)
    y_sum = ybuf[0]
    for d in range(1, n_dev):
        y_sum = y_sum + ybuf[d]
    for j in range(y_blocks):
        at = pl.ds(pl.multiple_of(me * y_cols + j * LANES, LANES), LANES)
        y_v[:, at] = (x_v[:, at].astype(f32) + y_sum[y_rows_at(j), :]).astype(bf16)
    send_all(y_v.at[:, half(me)], g_ssem, g_rsem)
    with jax.named_scope('g_recv'):
        wait_bytes(y_v.at[:, pl.ds(0, (n_dev - 1) * y_cols)], g_rsem)
    y_out[...] = y_v[...]

    for part in range(2):
        q_buf, _, _, obuf, _, _, mlbuf = part_refs[part][:7]
        n_heads = part_heads[part]
        wait_bytes(q_buf.at[pl.ds(0, (n_dev - 1) * n_heads)], q_ssem.at[part])
        wait_bytes(obuf.at[pl.ds(0, n_dev - 1)], o_ssem.at[part])
        wait_bytes(mlbuf.at[pl.ds(0, n_dev - 1)], ml_ssem.at[part])
    wait_bytes(kvbuf.at[pl.ds(0, n_dev - 1)], kv_ssem)
    wait_bytes(ybuf.at[pl.ds(0, n_dev - 1)], y_ssem)
    wait_bytes(y_v.at[:, pl.ds(0, (n_dev - 1) * y_cols)], g_ssem)


def store_kernel(*refs):
    sems, n_out = refs[-1], len(refs) // 2
    copies = [pltpu.make_async_copy(refs[i], refs[n_out + i], sems.at[i]) for i in range(n_out)]
    for c in copies:
        c.start()
    for c in copies:
        c.wait()


def solution(mesh):
    n_dev = mesh.shape["model"]

    def local_step(x, w_q, w_k, w_v, w_o, k_cache, v_cache, lengths):
        rows, _, t_local, head_dim = k_cache.shape
        depth = x.shape[1]
        own_heads = w_q.shape[1] // head_dim
        y_cols = w_o.shape[1] // n_dev
        chips = n_dev // 2
        f32, bf16 = jnp.float32, jnp.bfloat16

        def part_scratch(n_heads, batch):
            return [
                pltpu.VMEM((n_dev * n_heads, rows, head_dim), f32),
                pltpu.VMEM((rows, n_dev * n_heads, head_dim), f32),
                pltpu.VMEM((rows // batch, n_dev, batch * n_heads, head_dim), f32),
                pltpu.VMEM((n_dev, rows // batch, batch * n_heads, head_dim), f32),
                pltpu.VMEM((2, n_dev * n_heads, LANES), f32),
                pltpu.VMEM((n_dev, 2, n_heads, LANES), f32),
                pltpu.VMEM((n_dev, 2, n_heads, LANES), f32),
                pltpu.VMEM((rows, n_heads * head_dim), bf16),
                pltpu.VMEM((rows, n_heads, head_dim), f32),
            ]

        hbm = pl.BlockSpec(memory_space=pl.ANY)
        dma = pltpu.SemaphoreType.DMA
        vm = pl.BlockSpec(memory_space=pltpu.VMEM)
        y, k_new, v_new = pl.pallas_call(
            functools.partial(kernel, n_dev),
            out_shape=(pltpu.VMEM((rows, depth), bf16),
                       pltpu.VMEM((rows, head_dim), bf16),
                       pltpu.VMEM((rows, head_dim), bf16)),
            in_specs=[hbm] * 8,
            out_specs=(vm, vm, vm),
            scratch_shapes=[
                pltpu.SMEM((rows,), jnp.int32),
                pltpu.VMEM((rows, depth), bf16),
                pltpu.VMEM((w_o.shape[0] * w_o.shape[1] // WIDE, WIDE), bf16),
                pltpu.VMEM((2, depth // n_dev, head_dim), bf16),
                pltpu.VMEM((rows, t_local, head_dim), bf16),
                pltpu.VMEM((rows, t_local, head_dim), bf16),
                pltpu.VMEM((n_dev, 2, rows, head_dim), f32),
                pltpu.VMEM((3, FIRST * n_dev, t_local), f32),
                pltpu.VMEM((chips, rows, 2 * y_cols), f32),
                pltpu.VMEM((chips, 2, rows * y_cols // LANES, LANES), f32),
                pltpu.VMEM((n_dev, rows * y_cols // LANES, LANES), f32),
                pltpu.VMEM((rows, depth), bf16),
                *part_scratch(FIRST, SENDS[0]), *part_scratch(own_heads - FIRST, SENDS[1]),
                dma, dma, dma((RING,)), dma((2,)), dma((rows,)), dma((rows,)), dma((2, chips)),
            ] + [dma] * 6 + [dma((2,))] * 6,
            compiler_params=pltpu.CompilerParams(
                collective_id=0, has_side_effects=True, vmem_limit_bytes=63000000),
        )(x, w_q, w_k, w_v, w_o, k_cache, v_cache, lengths)
        outs = (y, k_new, v_new)
        return pl.pallas_call(
            store_kernel,
            out_shape=tuple(jax.ShapeDtypeStruct(o.shape, o.dtype) for o in outs),
            in_specs=[hbm] * 3,
            out_specs=(hbm,) * 3,
            scratch_shapes=[dma((len(outs),))],
            compiler_params=pltpu.CompilerParams(vmem_limit_bytes=1 << 20),
        )(*outs)

    row_spec = P("replica", None)
    cache_spec = P("replica", None, "model", None)
    return jax.shard_map(
        local_step, mesh=mesh,
        in_specs=(row_spec, P(None, "model"), P(), P(), P("model", None), cache_spec, cache_spec, P("replica")),
        out_specs=(row_spec, row_spec, row_spec), check_vma=False)
```

time: 37 us -> 35.8 us (0.968)
  Pallas kernels: 36.3 us -> 35.1 us
    pallas_call x1, Pallas kernels: 35.6 us -> 34.4 us  [local_step(): pl.pallas_call(functools.partial(kernel, n_dev), out_shape=(pltpu.VMEM((r...]
where the time goes in v4:
time: 35.8 us; the launch traced here: 35.7 us
  Pallas kernels  35.1 us (98%)
  between operations  0.64 us (2%)
    pallas_call x1, Pallas kernels, local_step(): pl.pallas_call(functools.partial(kernel, n_dev), out_shape=(pltpu.VMEM((r...  34.4 us

profile of v4, /device:TPU:0, one launch (start us, length us, event | category | flops | bytes accessed | tf_op | source)
XLA Modules:
  0.0 35.7 jit_solution(6843413928177281269)
XLA Ops:
  0.6 34.4 %shard_map.103 = (bf16[6,7168]{1,0:T(8,128)(2,1)S(1)}, bf16[6,256]{1,0:T(8,128)(2,1)S(1)}, bf16[6,256]{1,0:T(8,128)(2,1)S(1)}) custom-call(bf16[6,7168]{1,0:T(8,128)(2,1)} %x_hbm.1, bf16[7168,2048]{1,0:T(8,128)(2,1)} %wq_hbm.1, bf16[7168,256]{1,0:T(8,128)(2,1)} %wk_hbm.1, bf16[7168,256]{1,0:T(8,128)(2,1)} %wv_hbm.1, bf16[2048,7168]{1,0:T(8,128)(2,1)} %wo_hbm.1, ...), custom_call_target="tpu_custom_call" | custom-call | tf_op jit(solution)/shard_map/pallas_call | solution.py:371
  35.0 0.7 %shard_map.104 = (bf16[6,7168]{1,0:T(8,128)(2,1)}, bf16[6,256]{1,0:T(8,128)(2,1)}, bf16[6,256]{1,0:T(8,128)(2,1)}) custom-call(bf16[6,7168]{1,0:T(8,128)(2,1)S(1)} %get-tuple-element.6.refs_0_, bf16[6,256]{1,0:T(8,128)(2,1)S(1)} %get-tuple-element.7.refs_1_, bf16[6,256]{1,0:T(8,128)(2,1)S(1)} %get-tuple-element.8.refs_2_), custom_call_target="tpu_custom_call" | custom-call | tf_op jit(solution)/shard_map/pallas_call | solution.py:398

commit v5 on v4

--- a/solution.py
+++ b/solution.py
@@ -11,15 +11,14 @@
 RING = 4
 LANES = 128
 WIDE = 256
-FIRST = 5
-BATCH = 3
-SENDS = (3, 2)
+FIRST = 4
+SENDS = (2, 2)
 MESH = pl.DeviceIdType.MESH
 
 
 def kernel(n_dev, x_hbm, wq_hbm, wk_hbm, wv_hbm, wo_hbm, kc_hbm, vc_hbm, len_hbm,
            y_out, k_out, v_out,
-           len_s, x_v, w_v, wkv_v, k_v, v_v, kvbuf, s_buf, yacc, ysend, ybuf, y_v, *rest):
+           len_s, x_v, w_v, wkv_v, k_v, v_v, kt_v, kvbuf, s_buf, yacc, ysend, ybuf, y_v, *rest):
     part_refs, sems = (rest[:9], rest[9:18]), rest[18:]
     (len_sem, x_sem, wq_sem, wkv_sem, k_sem, v_sem, wo_sem,
      kv_ssem, kv_rsem, y_ssem, y_rsem, g_ssem, g_rsem, q_ssem, q_rsem, o_ssem, o_rsem, ml_ssem, ml_rsem) = sems
@@ -27,7 +26,6 @@
     head_dim = wk_hbm.shape[1]
     own_heads = wq_hbm.shape[1] // head_dim
     t_local = kc_hbm.shape[2]
-    kv_rows = depth // n_dev
     y_cols = wo_hbm.shape[1] // n_dev
     o_rows = wo_hbm.shape[0]
     chips = n_dev // 2
@@ -82,11 +80,10 @@
         for p in peers:
             send(ref, ref, ssem, rsem, p)
 
-    kv_slice = pl.ds(pl.multiple_of(me * kv_rows, LANES), kv_rows)
     x_copy = pltpu.make_async_copy(x_hbm, x_v, x_sem)
     len_copy = pltpu.make_async_copy(len_hbm, len_s, len_sem)
-    wk_copy = pltpu.make_async_copy(wk_hbm.at[kv_slice, :], wkv_v.at[0], wkv_sem.at[0])
-    wv_copy = pltpu.make_async_copy(wv_hbm.at[kv_slice, :], wkv_v.at[1], wkv_sem.at[1])
+    wk_copy = pltpu.make_async_copy(wk_hbm, wkv_v, wkv_sem)
+    wv_copy = pltpu.make_async_copy(wv_hbm, wkv_v, wkv_sem)
 
     def k_copy(b):
         return pltpu.make_async_copy(kc_hbm.at[b, 0], k_v.at[b], k_sem.at[b])
@@ -127,14 +124,16 @@
                 def _():
                     wq_copy(h + RING).start()
 
-            if h0 <= own_heads - RING < h0 + n_heads:
-                @pl.when(h == own_heads - RING)
+            if part == 1:
+                @pl.when((h == h0) & (me == 0))
                 def _():
                     wk_copy.start()
+
+                @pl.when((h == h0) & (me == 1))
+                def _():
                     wv_copy.start()
 
-            if h0 <= own_heads - RING + 1 < h0 + n_heads:
-                @pl.when(h == own_heads - RING + 1)
+                @pl.when(h == h0 + 1)
                 def _():
                     def start_kv(b, c):
                         k_copy(b).start()
@@ -167,29 +166,33 @@
 
         def scores(b):
             q_b = q_buf[:, b, :].astype(bf16)
-            s_buf[b % 3, 0:n_rows] = lax.dot_general(
-                q_b, k_v[b], (((1,), (1,)), ((), ())), preferred_element_type=f32)
-
-        def wait_kv(b0):
-            with jax.named_scope('kv_wait'):
-                for b in range(b0, b0 + BATCH):
-                    k_copy(b).wait()
-                    v_copy(b).wait()
+            if part == 0:
+                kt_v[b] = k_v[b].T
+                s_buf[b % 3] = lax.dot_general(
+                    q_b, k_v[b], (((1,), (1,)), ((), ())), preferred_element_type=f32)
+            else:
+                s_buf[b % 3] = jnp.dot(q_b, kt_v[b], preferred_element_type=f32)
 
         with jax.named_scope('q_recv'):
             wait_bytes(q_buf.at[pl.ds(0, n_rows - n_heads)], q_rsem.at[part])
+        m_all = jnp.zeros((n_rows, LANES), f32)
+        l_all = jnp.zeros((n_rows, LANES), f32)
         if part == 0:
             len_copy.wait()
-            wait_kv(0)
-        m_all = jnp.zeros((n_rows, LANES), f32)
-        l_all = jnp.zeros((n_rows, LANES), f32)
-        scores(0)
+        else:
+            scores(0)
+            scores(1)
         for b in range(rows):
-            if b + 1 < rows:
-                if part == 0 and (b + 1) % BATCH == 0:
-                    wait_kv(b + 1)
-                scores(b + 1)
-            s = jnp.where(positions < len_s[b], s_buf[b % 3, 0:n_rows], -jnp.inf)
+            if part == 0 and b % batch == 0:
+                with jax.named_scope('kv_wait'):
+                    for c in range(b, b + batch):
+                        k_copy(c).wait()
+                        v_copy(c).wait()
+                for c in range(b, b + batch):
+                    scores(c)
+            if part == 1 and b + 2 < rows:
+                scores(b + 2)
+            s = jnp.where(positions < len_s[b], s_buf[b % 3], -jnp.inf)
             m = jnp.max(s, axis=1, keepdims=True)
             m_safe = jnp.where(m == -jnp.inf, 0.0, m)
             p = jnp.exp2((s - m_safe) * factor)
@@ -215,25 +218,26 @@
         for d in peers:
             send(mlsend.at[d], mlbuf.at[me], ml_ssem.at[part], ml_rsem.at[part], d)
 
-    with jax.named_scope('wkv_wait'):
-        wk_copy.wait()
-        wv_copy.wait()
-    x_part = x_v[:, kv_slice]
-    for i in range(2):
-        kvbuf[me, i] = jnp.dot(x_part, wkv_v[i], preferred_element_type=f32)
-    send_all(kvbuf.at[me], kv_ssem, kv_rsem)
+    @pl.when(me < 2)
+    def _():
+        with jax.named_scope('wkv_wait'):
+            wk_copy.wait()
+        kv = jnp.dot(x_v[...], wkv_v[...], preferred_element_type=f32)
+        kvbuf[me] = kv.astype(bf16).astype(f32)
+        for p in peers:
+            send(kvbuf.at[me], kvbuf.at[me], kv_ssem, kv_rsem.at[me], p)
+
     attention(0)
     attention(1)
 
-    with jax.named_scope('kv_recv'):
-        wait_bytes(kvbuf.at[pl.ds(0, n_dev - 1)], kv_rsem)
-    kv_sum = kvbuf[0]
-    for d in range(1, n_dev):
-        kv_sum = kv_sum + kvbuf[d]
-    k_out[...] = kv_sum[0].astype(bf16)
-    v_out[...] = kv_sum[1].astype(bf16)
-    k_new = kv_sum[0].astype(bf16).astype(f32)
-    v_new = kv_sum[1].astype(bf16).astype(f32)
+    for i in range(2):
+        @pl.when(me != i)
+        def _():
+            with jax.named_scope('kv_recv'):
+                wait_bytes(kvbuf.at[i], kv_rsem.at[i])
+    k_new, v_new = kvbuf[0], kvbuf[1]
+    k_out[...] = k_new.astype(bf16)
+    v_out[...] = v_new.astype(bf16)
 
     def combine(part):
         q_buf, _, _, obuf, _, _, mlbuf, a_v, astage = part_refs[part]
@@ -290,13 +294,11 @@
 
     combine(0)
 
-    def y_first(g, c):
-        with jax.named_scope('wo_wait'):
+    with jax.named_scope('wo_wait'):
+        for g in range(chips):
             wait_group(0, g)
+    for g in range(chips):
         y_rows(0, g)
-        return c
-
-    lax.fori_loop(0, chips, y_first, 0)
     combine(1)
     last = chips - 1
     for g in range(chips):
@@ -327,7 +329,12 @@
         wait_bytes(q_buf.at[pl.ds(0, (n_dev - 1) * n_heads)], q_ssem.at[part])
         wait_bytes(obuf.at[pl.ds(0, n_dev - 1)], o_ssem.at[part])
         wait_bytes(mlbuf.at[pl.ds(0, n_dev - 1)], ml_ssem.at[part])
-    wait_bytes(kvbuf.at[pl.ds(0, n_dev - 1)], kv_ssem)
+
+    @pl.when(me < 2)
+    def _():
+        for p in peers:
+            wait_bytes(kvbuf.at[0], kv_ssem)
+
     wait_bytes(ybuf.at[pl.ds(0, n_dev - 1)], y_ssem)
     wait_bytes(y_v.at[:, pl.ds(0, (n_dev - 1) * y_cols)], g_ssem)
 
@@ -379,18 +386,20 @@
                 pltpu.SMEM((rows,), jnp.int32),
                 pltpu.VMEM((rows, depth), bf16),
                 pltpu.VMEM((w_o.shape[0] * w_o.shape[1] // WIDE, WIDE), bf16),
-                pltpu.VMEM((2, depth // n_dev, head_dim), bf16),
+                pltpu.VMEM((depth, head_dim), bf16),
                 pltpu.VMEM((rows, t_local, head_dim), bf16),
                 pltpu.VMEM((rows, t_local, head_dim), bf16),
-                pltpu.VMEM((n_dev, 2, rows, head_dim), f32),
+                pltpu.VMEM((rows, head_dim, t_local), bf16),
+                pltpu.VMEM((2, rows, head_dim), f32),
                 pltpu.VMEM((3, FIRST * n_dev, t_local), f32),
                 pltpu.VMEM((chips, rows, 2 * y_cols), f32),
                 pltpu.VMEM((chips, 2, rows * y_cols // LANES, LANES), f32),
                 pltpu.VMEM((n_dev, rows * y_cols // LANES, LANES), f32),
                 pltpu.VMEM((rows, depth), bf16),
                 *part_scratch(FIRST, SENDS[0]), *part_scratch(own_heads - FIRST, SENDS[1]),
-                dma, dma, dma((RING,)), dma((2,)), dma((rows,)), dma((rows,)), dma((2, chips)),
-            ] + [dma] * 6 + [dma((2,))] * 6,
+                dma, dma, dma((RING,)), dma, dma((rows,)), dma((rows,)), dma((2, chips)),
+                dma, dma((2,)),
+            ] + [dma] * 4 + [dma((2,))] * 6,
             compiler_params=pltpu.CompilerParams(
                 collective_id=0, has_side_effects=True, vmem_limit_bytes=63000000),
         )(x, w_q, w_k, w_v, w_o, k_cache, v_cache, lengths)

time: 35.8 us -> 33.9 us (0.947)
  Pallas kernels: 35.1 us -> 33.2 us
    pallas_call x1, Pallas kernels: 34.4 us -> 32.5 us  [local_step(): pl.pallas_call(functools.partial(kernel, n_dev), out_shape=(pltpu.VMEM((r...]
where the time goes in v5:
time: 33.9 us; the launch traced here: 33.8 us
  Pallas kernels  33.2 us (98%)
  between operations  0.64 us (2%)
    pallas_call x1, Pallas kernels, local_step(): pl.pallas_call(functools.partial(kernel, n_dev), out_shape=(pltpu.VMEM((r...  32.5 us
    pallas_call x1, Pallas kernels, local_step(): pl.pallas_call(store_kernel, out_shape=tuple((jax.ShapeDtypeStruct(o.shap...  0.68 us

profile of v5, /device:TPU:0, one launch (start us, length us, event | category | flops | bytes accessed | tf_op | source)
XLA Modules:
  0.0 33.8 jit_solution(4556997494285534549)
XLA Ops:
  0.6 32.5 %shard_map.103 = (bf16[6,7168]{1,0:T(8,128)(2,1)S(1)}, bf16[6,256]{1,0:T(8,128)(2,1)S(1)}, bf16[6,256]{1,0:T(8,128)(2,1)S(1)}) custom-call(bf16[6,7168]{1,0:T(8,128)(2,1)} %x_hbm.1, bf16[7168,2048]{1,0:T(8,128)(2,1)} %wq_hbm.1, bf16[7168,256]{1,0:T(8,128)(2,1)} %wk_hbm.1, bf16[7168,256]{1,0:T(8,128)(2,1)} %wv_hbm.1, bf16[2048,7168]{1,0:T(8,128)(2,1)} %wo_hbm.1, ...), custom_call_target="tpu_custom_call" | custom-call | tf_op jit(solution)/shard_map/pallas_call | solution.py:378
  33.1 0.7 %shard_map.104 = (bf16[6,7168]{1,0:T(8,128)(2,1)}, bf16[6,256]{1,0:T(8,128)(2,1)}, bf16[6,256]{1,0:T(8,128)(2,1)}) custom-call(bf16[6,7168]{1,0:T(8,128)(2,1)S(1)} %get-tuple-element.6.refs_0_, bf16[6,256]{1,0:T(8,128)(2,1)S(1)} %get-tuple-element.7.refs_1_, bf16[6,256]{1,0:T(8,128)(2,1)S(1)} %get-tuple-element.8.refs_2_), custom_call_target="tpu_custom_call" | custom-call | tf_op jit(solution)/shard_map/pallas_call | solution.py:407

commit v6 on v5

--- a/solution.py
+++ b/solution.py
@@ -12,13 +12,14 @@
 LANES = 128
 WIDE = 256
 FIRST = 4
-SENDS = (2, 2)
+CHUNK = 256
+PAIR = 2
 MESH = pl.DeviceIdType.MESH
 
 
 def kernel(n_dev, x_hbm, wq_hbm, wk_hbm, wv_hbm, wo_hbm, kc_hbm, vc_hbm, len_hbm,
            y_out, k_out, v_out,
-           len_s, x_v, w_v, wkv_v, k_v, v_v, kt_v, kvbuf, s_buf, yacc, ysend, ybuf, y_v, *rest):
+           len_s, x_v, w_v, wkv_v, k_v, v_v, kt_v, kvbuf, s_buf, p_buf, yacc, ysend, ybuf, y_v, *rest):
     part_refs, sems = (rest[:9], rest[9:18]), rest[18:]
     (len_sem, x_sem, wq_sem, wkv_sem, k_sem, v_sem, wo_sem,
      kv_ssem, kv_rsem, y_ssem, y_rsem, g_ssem, g_rsem, q_ssem, q_rsem, o_ssem, o_rsem, ml_ssem, ml_rsem) = sems
@@ -154,69 +155,112 @@
     positions = me * t_local + lax.broadcasted_iota(jnp.int32, (1, t_local), 1)
 
     def part_rows(part, b):
-        n = (b % SENDS[part]) * part_heads[part]
+        n = (b % PAIR) * part_heads[part]
         return slice(n, n + part_heads[part])
 
-    def attention(part):
-        q_buf, o_flat, osend, obuf, mlflat, mlsend, mlbuf = part_refs[part][:7]
+    chunks = [slice(c, c + CHUNK) for c in range(0, t_local, CHUNK)]
+    ml = [jnp.zeros((n * n_dev, LANES), f32) for n in part_heads]
+
+    def wait_q(part):
+        with jax.named_scope('q_recv'):
+            wait_bytes(part_refs[part][0].at[pl.ds(0, (n_dev - 1) * part_heads[part])], q_rsem.at[part])
+
+    def wait_kv(b):
+        with jax.named_scope('kv_wait'):
+            for c in range(b, b + PAIR):
+                k_copy(c).wait()
+                v_copy(c).wait()
+
+    def scores(b, parts, transposed):
+        q_b = jnp.concatenate([part_refs[p][0][:, b, :] for p in parts], axis=0).astype(bf16)
+        if transposed:
+            s = jnp.dot(q_b, kt_v[b], preferred_element_type=f32)
+        else:
+            s = lax.dot_general(q_b, k_v[b], (((1,), (1,)), ((), ())), preferred_element_type=f32)
+        s_buf[b % 3, :q_b.shape[0]] = s
+
+    def attend(b, parts):
+        n_rows = sum(part_heads[p] for p in parts) * n_dev
+
+        def masked(at):
+            return jnp.where(positions[:, at] < len_s[b], s_buf[b % 3, :n_rows, at], -jnp.inf)
+
+        m = functools.reduce(jnp.maximum, [masked(at) for at in chunks])
+        m = jnp.max(m, axis=1, keepdims=True)
+        m_safe = jnp.where(m == -jnp.inf, 0.0, m)
+        l = jnp.zeros((n_rows, CHUNK), f32)
+        for at in chunks:
+            p = jnp.exp2((masked(at) - m_safe) * factor)
+            l = l + p
+            hi = p.astype(bf16)
+            p_buf[b % 2, :n_rows, at] = hi
+            p_buf[b % 2, n_rows:2 * n_rows, at] = (p - hi.astype(f32)).astype(bf16)
+        l = jnp.sum(l, axis=1, keepdims=True)
+        o2 = jnp.dot(p_buf[b % 2, :2 * n_rows], v_v[b], preferred_element_type=f32)
+        o = o2[:n_rows] + o2[n_rows:]
+        row = 0
+        for part in parts:
+            n_heads = part_heads[part]
+            here = slice(row, row + n_heads * n_dev)
+            row += n_heads * n_dev
+            lane = lax.broadcasted_iota(jnp.int32, (n_heads * n_dev, LANES), 1)
+            ml[part] = jnp.where(lane == b, m[here], ml[part])
+            ml[part] = jnp.where(lane == b + LANES // 2, l[here], ml[part])
+            _, o_flat, osend = part_refs[part][:3]
+            o_flat[b] = o[here]
+            for d in range(n_dev):
+                osend[b // PAIR, d, part_rows(part, b), :] = o_flat[b, d * n_heads:(d + 1) * n_heads, :]
+
+    def send_ml(part):
+        mlflat, mlsend, mlbuf = part_refs[part][4:7]
         n_heads = part_heads[part]
-        n_rows = n_heads * n_dev
-        batch = SENDS[part]
-        lane = lax.broadcasted_iota(jnp.int32, (n_rows, LANES), 1)
-
-        def scores(b):
-            q_b = q_buf[:, b, :].astype(bf16)
-            if part == 0:
-                kt_v[b] = k_v[b].T
-                s_buf[b % 3] = lax.dot_general(
-                    q_b, k_v[b], (((1,), (1,)), ((), ())), preferred_element_type=f32)
-            else:
-                s_buf[b % 3] = jnp.dot(q_b, kt_v[b], preferred_element_type=f32)
-
-        with jax.named_scope('q_recv'):
-            wait_bytes(q_buf.at[pl.ds(0, n_rows - n_heads)], q_rsem.at[part])
-        m_all = jnp.zeros((n_rows, LANES), f32)
-        l_all = jnp.zeros((n_rows, LANES), f32)
-        if part == 0:
-            len_copy.wait()
-        else:
-            scores(0)
-            scores(1)
-        for b in range(rows):
-            if part == 0 and b % batch == 0:
-                with jax.named_scope('kv_wait'):
-                    for c in range(b, b + batch):
-                        k_copy(c).wait()
-                        v_copy(c).wait()
-                for c in range(b, b + batch):
-                    scores(c)
-            if part == 1 and b + 2 < rows:
-                scores(b + 2)
-            s = jnp.where(positions < len_s[b], s_buf[b % 3], -jnp.inf)
-            m = jnp.max(s, axis=1, keepdims=True)
-            m_safe = jnp.where(m == -jnp.inf, 0.0, m)
-            p = jnp.exp2((s - m_safe) * factor)
-            l = jnp.sum(p, axis=1, keepdims=True)
-            hi = p.astype(bf16).astype(f32)
-            terms = jnp.concatenate([hi, p - hi], axis=0).astype(bf16)
-            o2 = jnp.dot(terms, v_v[b], preferred_element_type=f32)
-            o_flat[b] = o2[:n_rows] + o2[n_rows:]
-            m_all = jnp.where(lane == b, m, m_all)
-            l_all = jnp.where(lane == b, l, l_all)
-            for d in range(n_dev):
-                osend[b // batch, d, part_rows(part, b), :] = o_flat[b, d * n_heads:(d + 1) * n_heads, :]
-            if (b + 1) % batch == 0:
-                n = b // batch
-                obuf[me, n] = osend[n, me]
-                for d in peers:
-                    send(osend.at[n, d], obuf.at[me, n], o_ssem.at[part], o_rsem.at[part], d)
-        mlflat[0] = m_all
-        mlflat[1] = l_all
+        mlflat[...] = ml[part]
         for d in range(n_dev):
-            mlsend[d] = mlflat[:, d * n_heads:(d + 1) * n_heads, :]
+            mlsend[d] = mlflat[d * n_heads:(d + 1) * n_heads, :]
         mlbuf[me] = mlsend[me]
         for d in peers:
             send(mlsend.at[d], mlbuf.at[me], ml_ssem.at[part], ml_rsem.at[part], d)
+
+    def send_o(part, n):
+        _, _, osend, obuf = part_refs[part][:4]
+        obuf[me, n] = osend[n, me]
+        for d in peers:
+            send(osend.at[n, d], obuf.at[me, n], o_ssem.at[part], o_rsem.at[part], d)
+
+    tail = rows - PAIR
+
+    def attention_first():
+        wait_q(0)
+        len_copy.wait()
+        for b in range(0, tail, PAIR):
+            wait_kv(b)
+            for c in range(b, b + PAIR):
+                kt_v[c] = k_v[c].T
+                scores(c, (0,), False)
+            for c in range(b, b + PAIR):
+                attend(c, (0,))
+            send_o(0, b // PAIR)
+
+    def attention_second():
+        wait_q(1)
+        wait_kv(tail)
+        for c in range(tail, rows):
+            scores(c, (0, 1), False)
+        for c in range(tail, rows):
+            attend(c, (0, 1))
+        send_ml(0)
+        send_o(0, tail // PAIR)
+        send_o(1, tail // PAIR)
+        for c in range(PAIR):
+            scores(c, (1,), True)
+        for b in range(tail):
+            if b + PAIR < tail:
+                scores(b + PAIR, (1,), True)
+            attend(b, (1,))
+            if (b + 1) % PAIR == 0:
+                if b + 1 == tail:
+                    send_ml(1)
+                send_o(1, b // PAIR)
 
     @pl.when(me < 2)
     def _():
@@ -227,8 +271,8 @@
         for p in peers:
             send(kvbuf.at[me], kvbuf.at[me], kv_ssem, kv_rsem.at[me], p)
 
-    attention(0)
-    attention(1)
+    attention_first()
+    attention_second()
 
     for i in range(2):
         @pl.when(me != i)
@@ -243,28 +287,29 @@
         q_buf, _, _, obuf, _, _, mlbuf, a_v, astage = part_refs[part]
         n_heads = part_heads[part]
         lane = lax.broadcasted_iota(jnp.int32, (n_heads, LANES), 1)
-        with jax.named_scope('o_recv'):
+        with jax.named_scope('ml_recv'):
             wait_bytes(mlbuf.at[pl.ds(0, n_dev - 1)], ml_rsem.at[part])
-            wait_bytes(obuf.at[pl.ds(0, n_dev - 1)], o_rsem.at[part])
         s_new = jnp.zeros((n_heads, LANES), f32)
         for b in range(rows):
             q_own = q_buf[pl.ds(me * n_heads, n_heads), b, :]
             s_new = jnp.where(lane == b, jnp.sum(q_own * k_new[b:b + 1, :], axis=1, keepdims=True), s_new)
         top = s_new
         for d in range(n_dev):
-            top = jnp.maximum(top, mlbuf[d, 0])
+            top = jnp.maximum(top, mlbuf[d])
         w_new = jnp.exp2((s_new - top) * factor)
-        w = [jnp.exp2((mlbuf[d, 0] - top) * factor) for d in range(n_dev)]
+        w = [jnp.exp2((mlbuf[d] - top) * factor) for d in range(n_dev)]
         total = w_new
         for d in range(n_dev):
-            total = total + w[d] * mlbuf[d, 1]
+            total = total + w[d] * pltpu.roll(mlbuf[d], LANES // 2, 1)
         inv = 1.0 / total
         w_new = w_new * inv
         w = [w_d * inv for w_d in w]
+        with jax.named_scope('o_recv'):
+            wait_bytes(obuf.at[pl.ds(0, n_dev - 1)], o_rsem.at[part])
         for b in range(rows):
             acc = w_new[:, b:b + 1] * v_new[b:b + 1, :]
             for d in range(n_dev):
-                acc = acc + w[d][:, b:b + 1] * obuf[d, b // SENDS[part], part_rows(part, b), :]
+                acc = acc + w[d][:, b:b + 1] * obuf[d, b // PAIR, part_rows(part, b), :]
             astage[b] = acc
         for h in range(n_heads):
             a_v[:, h * head_dim:(h + 1) * head_dim] = astage[:, h, :].astype(bf16)
@@ -274,40 +319,44 @@
     def y_rows_at(block):
         return slice(block * rows, (block + 1) * rows)
 
-    def y_rows(part, g):
-        a_v = part_refs[part][7]
-        size = part_heads[part] * head_dim
-        for i in range(pieces):
-            row = pl.multiple_of((g * pieces + i) * o_rows + part_row0[part], 256)
-            y = jnp.dot(a_v[...], w_v[pl.ds(row, size), :], preferred_element_type=f32)
-            at = slice(i * WIDE, (i + 1) * WIDE)
-            if part == 0:
-                yacc[g, :, at] = y
-                continue
-            y = yacc[g, :, at] + y
-            for j in range(WIDE // LANES):
-                block = i * (WIDE // LANES) + j
-                ysend[g, block // y_blocks, y_rows_at(block % y_blocks), :] = y[:, j * LANES:(j + 1) * LANES]
+    def y_dot(g, i, parts):
+        a = jnp.concatenate([part_refs[p][7][...] for p in parts], axis=1)
+        row = (g * pieces + i) * o_rows + part_row0[parts[0]]
+        return jnp.dot(a, w_v[pl.ds(row, a.shape[1]), :], preferred_element_type=f32)
+
+    def y_store(g, i, y):
+        for j in range(WIDE // LANES):
+            block = i * (WIDE // LANES) + j
+            ysend[g, block // y_blocks, y_rows_at(block % y_blocks), :] = y[:, j * LANES:(j + 1) * LANES]
+
+    def piece_cols(i):
+        return slice(i * WIDE, (i + 1) * WIDE)
 
     def half(h):
         return pl.ds(pl.multiple_of(h * y_cols, LANES), y_cols)
 
     combine(0)
 
+    last = chips - 1
     with jax.named_scope('wo_wait'):
-        for g in range(chips):
+        for g in range(last):
             wait_group(0, g)
-    for g in range(chips):
-        y_rows(0, g)
+    for g in range(last):
+        for i in range(pieces):
+            yacc[g, :, piece_cols(i)] = y_dot(g, i, (0,))
     combine(1)
-    last = chips - 1
-    for g in range(chips):
+    for g in range(last):
         with jax.named_scope('wo_wait'):
             wait_group(1, g)
-        y_rows(1, g)
-        if g < last:
-            for k in range(2):
-                send(ysend.at[g, k], ybuf.at[me], y_ssem, y_rsem, 2 * group_chip[g] + k)
+        for i in range(pieces):
+            y_store(g, i, yacc[g, :, piece_cols(i)] + y_dot(g, i, (1,)))
+        for k in range(2):
+            send(ysend.at[g, k], ybuf.at[me], y_ssem, y_rsem, 2 * group_chip[g] + k)
+    with jax.named_scope('wo_wait'):
+        wait_group(0, last)
+        wait_group(1, last)
+    for i in range(pieces):
+        y_store(last, i, y_dot(last, i, (0, 1)))
     send(ysend.at[last, 1 - core], ybuf.at[me], y_ssem, y_rsem, peers[-1])
     ybuf[me] = ysend[last, core]
     with jax.named_scope('y_recv'):
@@ -319,10 +368,6 @@
         at = pl.ds(pl.multiple_of(me * y_cols + j * LANES, LANES), LANES)
         y_v[:, at] = (x_v[:, at].astype(f32) + y_sum[y_rows_at(j), :]).astype(bf16)
     send_all(y_v.at[:, half(me)], g_ssem, g_rsem)
-    with jax.named_scope('g_recv'):
-        wait_bytes(y_v.at[:, pl.ds(0, (n_dev - 1) * y_cols)], g_rsem)
-    y_out[...] = y_v[...]
-
     for part in range(2):
         q_buf, _, _, obuf, _, _, mlbuf = part_refs[part][:7]
         n_heads = part_heads[part]
@@ -337,6 +382,9 @@
 
     wait_bytes(ybuf.at[pl.ds(0, n_dev - 1)], y_ssem)
     wait_bytes(y_v.at[:, pl.ds(0, (n_dev - 1) * y_cols)], g_ssem)
+    with jax.named_scope('g_recv'):
+        wait_bytes(y_v.at[:, pl.ds(0, (n_dev - 1) * y_cols)], g_rsem)
+    y_out[...] = y_v[...]
 
 
 def store_kernel(*refs):
@@ -359,15 +407,15 @@
         chips = n_dev // 2
         f32, bf16 = jnp.float32, jnp.bfloat16
 
-        def part_scratch(n_heads, batch):
+        def part_scratch(n_heads):
             return [
                 pltpu.VMEM((n_dev * n_heads, rows, head_dim), f32),
                 pltpu.VMEM((rows, n_dev * n_heads, head_dim), f32),
-                pltpu.VMEM((rows // batch, n_dev, batch * n_heads, head_dim), f32),
-                pltpu.VMEM((n_dev, rows // batch, batch * n_heads, head_dim), f32),
-                pltpu.VMEM((2, n_dev * n_heads, LANES), f32),
-                pltpu.VMEM((n_dev, 2, n_heads, LANES), f32),
-                pltpu.VMEM((n_dev, 2, n_heads, LANES), f32),
+                pltpu.VMEM((rows // PAIR, n_dev, PAIR * n_heads, head_dim), f32),
+                pltpu.VMEM((n_dev, rows // PAIR, PAIR * n_heads, head_dim), f32),
+                pltpu.VMEM((n_dev * n_heads, LANES), f32),
+                pltpu.VMEM((n_dev, n_heads, LANES), f32),
+                pltpu.VMEM((n_dev, n_heads, LANES), f32),
                 pltpu.VMEM((rows, n_heads * head_dim), bf16),
                 pltpu.VMEM((rows, n_heads, head_dim), f32),
             ]
@@ -391,12 +439,13 @@
                 pltpu.VMEM((rows, t_local, head_dim), bf16),
                 pltpu.VMEM((rows, head_dim, t_local), bf16),
                 pltpu.VMEM((2, rows, head_dim), f32),
-                pltpu.VMEM((3, FIRST * n_dev, t_local), f32),
-                pltpu.VMEM((chips, rows, 2 * y_cols), f32),
+                pltpu.VMEM((3, own_heads * n_dev, t_local), f32),
+                pltpu.VMEM((2, 2 * own_heads * n_dev, t_local), bf16),
+                pltpu.VMEM((chips - 1, rows, 2 * y_cols), f32),
                 pltpu.VMEM((chips, 2, rows * y_cols // LANES, LANES), f32),
                 pltpu.VMEM((n_dev, rows * y_cols // LANES, LANES), f32),
                 pltpu.VMEM((rows, depth), bf16),
-                *part_scratch(FIRST, SENDS[0]), *part_scratch(own_heads - FIRST, SENDS[1]),
+                *part_scratch(FIRST), *part_scratch(own_heads - FIRST),
                 dma, dma, dma((RING,)), dma, dma((rows,)), dma((rows,)), dma((2, chips)),
                 dma, dma((2,)),
             ] + [dma] * 4 + [dma((2,))] * 6,

time: 33.9 us -> 32.9 us (0.971)
  Pallas kernels: 33.2 us -> 32.2 us
    pallas_call x1, Pallas kernels: 32.5 us -> 31.5 us  [local_step(): pl.pallas_call(functools.partial(kernel, n_dev), out_shape=(pltpu.VMEM((r...]
where the time goes in v6:
time: 32.9 us; the launch traced here: 32.8 us
  Pallas kernels  32.2 us (98%)
  between operations  0.64 us (2%)
    pallas_call x1, Pallas kernels, local_step(): pl.pallas_call(functools.partial(kernel, n_dev), out_shape=(pltpu.VMEM((r...  31.5 us
    pallas_call x1, Pallas kernels, local_step(): pl.pallas_call(store_kernel, out_shape=tuple((jax.ShapeDtypeStruct(o.shap...  0.68 us

profile of v6, /device:TPU:0, one launch (start us, length us, event | category | flops | bytes accessed | tf_op | source)
XLA Modules:
  0.0 32.8 jit_solution(6267952981076989378)
XLA Ops:
  0.6 31.5 %shard_map.103 = (bf16[6,7168]{1,0:T(8,128)(2,1)S(1)}, bf16[6,256]{1,0:T(8,128)(2,1)S(1)}, bf16[6,256]{1,0:T(8,128)(2,1)S(1)}) custom-call(bf16[6,7168]{1,0:T(8,128)(2,1)} %x_hbm.1, bf16[7168,2048]{1,0:T(8,128)(2,1)} %wq_hbm.1, bf16[7168,256]{1,0:T(8,128)(2,1)} %wk_hbm.1, bf16[7168,256]{1,0:T(8,128)(2,1)} %wv_hbm.1, bf16[2048,7168]{1,0:T(8,128)(2,1)} %wo_hbm.1, ...), custom_call_target="tpu_custom_call" | custom-call | tf_op jit(solution)/shard_map/pallas_call | solution.py:426
  32.2 0.7 %shard_map.104 = (bf16[6,7168]{1,0:T(8,128)(2,1)}, bf16[6,256]{1,0:T(8,128)(2,1)}, bf16[6,256]{1,0:T(8,128)(2,1)}) custom-call(bf16[6,7168]{1,0:T(8,128)(2,1)S(1)} %get-tuple-element.6.refs_0_, bf16[6,256]{1,0:T(8,128)(2,1)S(1)} %get-tuple-element.7.refs_1_, bf16[6,256]{1,0:T(8,128)(2,1)S(1)} %get-tuple-element.8.refs_2_), custom_call_target="tpu_custom_call" | custom-call | tf_op jit(solution)/shard_map/pallas_call | solution.py:456
